TPU v7x, 32 devices: a 4x4x1 block of a 4x4x8 slice. The times are simulated.
32 devices in a mesh: dp: 1 (over z), tp: 4 (over y), ep: 8 (over x, core).
Axes of the slice: x: 4, y: 4, z: 1, core: 2. Of those that a mesh axis runs over, the one named last changes fastest.
The devices are a block of a 4x4x8 slice.
Arguments:
- hidden_in: bfloat16 [8, 1024, 4096], P(('dp', 'ep'))
- expert_ids: int32 [8, 1024, 2], P(('dp', 'ep'))
- slot_ids: int32 [8, 1024, 2], P(('dp', 'ep'))
- attn_gain: bfloat16 [4096], replicated
- w_query: bfloat16 [4096, 32, 128], P(None, 'tp')
- w_key: bfloat16 [4096, 32, 128], P(None, 'tp')
- w_value: bfloat16 [4096, 32, 128], P(None, 'tp')
- w_out: bfloat16 [32, 128, 4096], P('tp')
- ffn_gain: bfloat16 [4096], replicated
- w_gate: bfloat16 [4096, 11008], P(None, 'tp')
- w_up: bfloat16 [4096, 11008], P(None, 'tp')
- w_down: bfloat16 [11008, 4096], P('tp')
- moe_gain: bfloat16 [4096], replicated
- w_router: bfloat16 [4096, 8], replicated
- exp_gate: bfloat16 [8, 4096, 1376], P('ep')
- exp_up: bfloat16 [8, 4096, 1376], P('ep')
- exp_down: bfloat16 [8, 1376, 4096], P('ep')
Outputs:
- output: bfloat16 [8, 1024, 4096], P(('dp', 'ep'))
All inputs are finite; a program needn't handle non-finite values.
Results may differ from a plain program's by a relative error of at most 0.00953262.
Values are sent between devices in bfloat16 or wider.
A program may use at most 768 MiB of HBM per device.

v0:
```python
import jax
import jax.numpy as jnp
from jax import lax
from jax.sharding import PartitionSpec as P

EPS = 1e-6
ROPE_BASE = 10000.0


def rms_norm(x_val, gain):
    x_f32 = x_val.astype(jnp.float32)
    inv_rms = lax.rsqrt(jnp.mean(x_f32 * x_f32, axis=-1, keepdims=True) + EPS)
    return (x_f32 * inv_rms * gain.astype(jnp.float32)).astype(jnp.bfloat16)


def rope_tables(seq_len, head_dim):
    inv_freq = ROPE_BASE ** (-jnp.arange(head_dim // 2, dtype=jnp.float32) * (2.0 / head_dim))
    angle = jnp.arange(seq_len, dtype=jnp.float32)[:, None] * inv_freq[None, :]
    return jnp.cos(angle), jnp.sin(angle)


def apply_rope(x_val, cos_tab, sin_tab):
    half_dim = x_val.shape[-1] // 2
    lower = x_val[..., :half_dim]
    upper = x_val[..., half_dim:]
    cos_b = cos_tab[:, None, :]
    sin_b = sin_tab[:, None, :]
    return jnp.concatenate([lower * cos_b - upper * sin_b, upper * cos_b + lower * sin_b], axis=-1)


def dense_branch(hidden, attn_gain, w_query, w_key, w_value, w_out, ffn_gain, w_gate, w_up, w_down):
    num_seqs, seq_len, d_model = hidden.shape
    head_dim = w_query.shape[2]
    x_norm = rms_norm(hidden, attn_gain)
    cos_tab, sin_tab = rope_tables(seq_len, head_dim)
    query = apply_rope(jnp.einsum('bsd,dhe->bshe', x_norm, w_query, preferred_element_type=jnp.float32), cos_tab, sin_tab).astype(jnp.bfloat16)
    key_proj = apply_rope(jnp.einsum('bsd,dhe->bshe', x_norm, w_key, preferred_element_type=jnp.float32), cos_tab, sin_tab).astype(jnp.bfloat16)
    value_proj = jnp.einsum('bsd,dhe->bshe', x_norm, w_value, preferred_element_type=jnp.float32).astype(jnp.bfloat16)
    scores = jnp.einsum('bqhe,bkhe->bhqk', query, key_proj, preferred_element_type=jnp.float32) * head_dim ** -0.5
    causal = jnp.arange(seq_len)[:, None] >= jnp.arange(seq_len)[None, :]
    attn_prob = jax.nn.softmax(jnp.where(causal, scores, -1e30), axis=-1).astype(jnp.bfloat16)
    context = jnp.einsum('bhqk,bkhe->bqhe', attn_prob, value_proj, preferred_element_type=jnp.float32).astype(jnp.bfloat16)
    attn_part = jnp.einsum('crif,ife->cre', context, w_out, preferred_element_type=jnp.float32)
    attn_sum = lax.psum(attn_part, 'tp')
    after_attn = (hidden.astype(jnp.float32) + attn_sum).astype(jnp.bfloat16)
    f_norm = rms_norm(after_attn, ffn_gain).reshape(num_seqs * seq_len, d_model)
    gate_pre = jnp.dot(f_norm, w_gate, preferred_element_type=jnp.float32)
    up_pre = jnp.dot(f_norm, w_up, preferred_element_type=jnp.float32)
    hidden_act = (jax.nn.silu(gate_pre) * up_pre).astype(jnp.bfloat16)
    ffn_part = jnp.dot(hidden_act, w_down, preferred_element_type=jnp.float32)
    ffn_sum = lax.psum(ffn_part, 'tp').reshape(num_seqs, seq_len, d_model)
    return after_attn.astype(jnp.float32) + ffn_sum


def expert_swiglu(x_buf, exp_gate, exp_up, exp_down):
    gate_pre = jnp.einsum('erd,edf->erf', x_buf, exp_gate, preferred_element_type=jnp.float32)
    up_pre = jnp.einsum('erd,edf->erf', x_buf, exp_up, preferred_element_type=jnp.float32)
    hidden_act = (jax.nn.silu(gate_pre) * up_pre).astype(jnp.bfloat16)
    return jnp.einsum('erf,efd->erd', hidden_act, exp_down, preferred_element_type=jnp.float32).astype(jnp.bfloat16)


def moe_branch(hidden, expert_ids, slot_ids, moe_gain, w_router, exp_gate, exp_up, exp_down):
    num_seqs, seq_len, d_model = hidden.shape
    tok_dev = num_seqs * seq_len
    top_k = expert_ids.shape[2]
    experts = w_router.shape[1]
    capacity = 3 * tok_dev * top_k // (2 * experts)
    u_norm = rms_norm(hidden, moe_gain).reshape(tok_dev, d_model)
    route_ids = expert_ids.reshape(tok_dev, top_k)
    logits = jnp.dot(u_norm, w_router, preferred_element_type=jnp.float32)
    gates = jax.nn.softmax(jnp.take_along_axis(logits, route_ids, axis=1), axis=-1)
    flat_pos = route_ids * capacity + slot_ids.reshape(tok_dev, top_k)
    token_of = jnp.broadcast_to(jnp.arange(tok_dev, dtype=jnp.int32)[:, None], (tok_dev, top_k))
    row_token = jnp.full((experts * capacity,), tok_dev, jnp.int32).at[flat_pos.reshape(-1)].set(token_of.reshape(-1))
    send_buf = jnp.take(u_norm, row_token, axis=0, mode='fill', fill_value=0).reshape(experts, capacity, d_model)
    recv_buf = lax.all_to_all(send_buf, 'ep', 0, 1, tiled=True)
    expert_out = expert_swiglu(recv_buf, exp_gate, exp_up, exp_down)
    returned = lax.all_to_all(expert_out, 'ep', 1, 0, tiled=True).reshape(experts * capacity, d_model)
    per_copy = jnp.take(returned, flat_pos, axis=0)
    moe_out = jnp.sum(gates[:, :, None] * per_copy.astype(jnp.float32), axis=1)
    return moe_out.reshape(num_seqs, seq_len, d_model)


def solution(mesh):
    tok_spec = P(('dp', 'ep'), None, None)
    col_spec = P(None, 'tp', None)
    exp_spec = P('ep', None, None)
    in_specs = (tok_spec, tok_spec, tok_spec, P(None), col_spec, col_spec, col_spec, P('tp', None, None), P(None), P(None, 'tp'), P(None, 'tp'), P('tp', None), P(None), P(None, None), exp_spec, exp_spec, exp_spec)

    def layer_local(hidden_in, expert_ids, slot_ids, attn_gain, w_query, w_key, w_value, w_out, ffn_gain, w_gate, w_up, w_down, moe_gain, w_router, exp_gate, exp_up, exp_down):
        moe_out = moe_branch(hidden_in, expert_ids, slot_ids, moe_gain, w_router, exp_gate, exp_up, exp_down)
        dense_out = dense_branch(hidden_in, attn_gain, w_query, w_key, w_value, w_out, ffn_gain, w_gate, w_up, w_down)
        return (dense_out + moe_out).astype(jnp.bfloat16)

    return jax.shard_map(layer_local, mesh=mesh, in_specs=in_specs, out_specs=tok_spec, check_vma=False)
```

profile of v0, /device:TPU:97, one launch (start us, length us, event | category | flops | bytes accessed | tf_op | source)
XLA Modules:
  0.0 1698.2 jit_solution(17240878841555601529)
XLA Ops:
  6.6 1.3 iota_compare_fusion
  7.9 5.1 fusion.6
  13.0 0.7 convert_element_type.75
  13.7 11.9 copy.53
  25.6 12.0 copy.52
  37.6 13.0 fusion.27
  50.7 13.2 fusion.25
  63.9 1.0 fusion.50
  64.9 14.0 fusion.23
  78.9 3.3 fusion.42
  82.2 14.2 fusion.77
  96.4 19.3 %fusion.16 = bf16[8,128,1024]{2,1,0:T(8,128)(2,1)} fusion(f32[8,1024]{1,0:T(8,128)S(1)} %fusion.77, pred[1024,1024]{0,1:T(8,128)(4,1)} %iota_compare_fusion, bf16[1024,8,128]{2,0,1:T(8,128)(2,1)} %fusion.23, bf16[1024,8,64]{0,2,1:T(8,128)(2,1)} %get-tuple-element.12, bf16[1024,8,64]{0,2,1:T(8,128)(2,1)} %get-tuple-element.13, ...), kind=kOutput, calls=%fused_computation.35 | convolution fusion | flops 4345308160 | bytes 9469952 | tf_op jit(solution)/shard_map/bhqk,bkhe->bqhe/dot_general | solution.py:42
  115.7 16.5 convolution_bitcast_fusion.1
  132.3 0.6 copy-done.13
  133.9 8.1 scatter_custom_fusion
  142.0 284.3 %all-reduce.3.cloned.1.call-done = f32[1,1024,4096]{2,1,0:T(8,128)} async-done(((f32[1,1024,4096]{2,1,0:T(8,128)}), f32[1,1024,4096]{2,1,0:T(8,128)}) %all-reduce.3.cloned.1.call-update) | async-done | bytes 16777232 | tf_op jit(solution)/shard_map/psum | solution.py:44
  426.3 15.9 fusion.8
  442.2 46.7 %gather_fusion = bf16[3072,4096]{1,0:T(8,128)(2,1)} fusion(bf16[1024,4096]{1,0:T(8,128)(2,1)} %get-tuple-element.7, s32[3072]{0:T(1024)S(1)} %fusion.51), kind=kCustom, calls=%fused_computation | custom fusion | bytes 50343936 | tf_op jit(solution)/shard_map/jit(_take)/gather | solution.py:75
  489.0 20.8 %broadcast_select_fusion.1 = bf16[8,384,4096]{2,1,0:T(8,128)(2,1)} fusion(bf16[8,384,4096]{2,1,0:T(8,128)(2,1)} %bitcast.115, pred[8,384]{1,0:T(8,128)(4,1)S(1)} %broadcast_in_dim.67), kind=kLoop, calls=%fused_computation.19 | loop fusion | flops 12582912 | bytes 50334720 | tf_op jit(solution)/shard_map/jit(_take)/select_n | solution.py:75
  509.8 7.8 all-to-all-start
  517.6 0.6 convert_element_type.84
  518.2 0.6 add_rsqrt_fusion
  518.8 272.0 %all-to-all-done = bf16[8,384,4096]{2,1,0:T(8,128)(2,1)} async-done(((bf16[8,384,4096]{2,1,0:T(8,128)(2,1)}), bf16[8,384,4096]{2,1,0:T(8,128)(2,1)}, u32[]{:S(2)}, u32[]{:S(2)}) %all-to-all-start) | async-done | bytes 25165856 | tf_op jit(solution)/shard_map/all_to_all | solution.py:76
  790.9 44.2 %fusion.19 = f32[3072,1376]{0,1:T(8,128)} fusion(bf16[3072,4096]{1,0:T(8,128)(2,1)} %bitcast.27, bf16[1,4096,1376]{1,2,0:T(8,128)(2,1)} %param.31), kind=kOutput, calls=%fused_computation.38 | convolution fusion | flops 34628173824 | bytes 53346304 | tf_op jit(solution)/shard_map/erd,edf->erf/dot_general | solution.py:56
  835.1 44.5 %multiply_convert_fusion = bf16[3072,1376]{0,1:T(8,128)(2,1)} fusion(f32[3072,1376]{0,1:T(8,128)} %fusion.19, bf16[3072,4096]{1,0:T(8,128)(2,1)} %bitcast.27, bf16[1,4096,1376]{1,2,0:T(8,128)(2,1)S(1)} %bitcast.124), kind=kOutput, calls=%fused_computation.22 | convolution fusion | flops 34653536256 | bytes 61800448 | tf_op jit(solution)/shard_map/erd,edf->erf/dot_general | solution.py:57
  879.6 44.9 %convert_bitcast_fusion = bf16[1,3072,4096]{2,1,0:T(8,128)(2,1)S(1)} fusion(bf16[3072,1376]{0,1:T(8,128)(2,1)} %multiply_convert_fusion, bf16[1,1376,4096]{2,1,0:T(8,128)(2,1)} %param.33), kind=kOutput, calls=%fused_computation.12 | convolution fusion | flops 34640756736 | bytes 44892160 | tf_op jit(solution)/shard_map/erf,efd->erd/dot_general | solution.py:59
  924.5 57.9 %copy.76 = bf16[1,3072,4096]{2,0,1:T(2,128)(2,1)} copy(bf16[1,3072,4096]{2,1,0:T(8,128)(2,1)S(1)} %convert_bitcast_fusion) | data formatting | bytes 50331648 | tf_op jit(solution)/shard_map/convert_element_type | solution.py:59
  982.4 0.6 broadcast.248
  983.0 152.2 %reduce.6 = bf16[3072,4096]{1,0:T(8,128)(2,1)} reduce(bf16[3072,1,4096]{2,1,0:T(2,128)(2,1)} %bitcast.113, bf16[]{:T(256)} %broadcast.248), dimensions={1}, to_apply=%bitcast.111.reduce_sub_computation | reduce | bytes 50331648
  1135.2 24.4 %reshape.434 = bf16[8,2,786432]{2,1,0:T(2,128)(2,1)} reshape(bf16[3072,4096]{1,0:T(8,128)(2,1)} %reduce.6) | data formatting | bytes 50331648
  1159.6 7.5 all-to-all-start.1
  1167.1 31.0 %fusion.37 = f32[1024,2752]{0,1:T(8,128)} fusion(bf16[4096,2752]{0,1:T(8,128)(2,1)} %param.26, bf16[1,1024,4096]{2,1,0:T(8,128)(2,1)} %get-tuple-element.6, f32[4096]{0:T(1024)S(1)} %copy-done.12, f32[1024]{0:T(1024)S(1)} %copy-done.15), kind=kOutput, calls=%fused_computation.54 | convolution fusion | flops 23102226432 | bytes 42225664 | tf_op jit(solution)/shard_map/dot_general | solution.py:47
  1198.1 31.1 %multiply_convert_fusion.1 = bf16[1024,2752]{0,1:T(8,128)(2,1)S(1)} fusion(f32[1024,2752]{0,1:T(8,128)} %fusion.37, bf16[4096,2752]{0,1:T(8,128)(2,1)} %param.27, bf16[1,1024,4096]{2,1,0:T(8,128)(2,1)} %get-tuple-element.6, f32[4096]{0:T(1024)S(1)} %copy-done.12, f32[1024]{0:T(1024)S(1)} %copy-done.15), kind=kOutput, calls=%fused_computation.40 | convolution fusion | flops 23119134720 | bytes 47861760 | tf_op jit(solution)/shard_map/dot_general | solution.py:48
  1229.2 30.2 %convolution_bitcast_fusion = f32[1,1024,4096]{2,1,0:T(8,128)} fusion(bf16[1024,2752]{0,1:T(8,128)(2,1)S(1)} %multiply_convert_fusion.1, bf16[2752,4096]{1,0:T(8,128)(2,1)} %param.28), kind=kOutput, calls=%fused_computation.41 | convolution fusion | flops 23085449216 | bytes 44957696 | tf_op jit(solution)/shard_map/dot_general | solution.py:50
  1259.5 0.6 copy-done.11
  1261.6 0.6 broadcast_clamp_fusion
  1262.2 0.8 compare_and_fusion
  1263.1 5.6 fusion.78
  1268.7 12.5 gather_fusion.2
  1281.2 0.5 reshape.413
  1282.0 0.4 fusion.48
  1282.7 157.8 %all-to-all-done.1 = bf16[8,2,786432]{2,1,0:T(2,128)(2,1)} async-done(((bf16[8,2,786432]{2,1,0:T(2,128)(2,1)}), bf16[8,2,786432]{2,1,0:T(2,128)(2,1)}, u32[]{:S(2)}, u32[]{:S(2)}) %all-to-all-start.1) | async-done | bytes 25165856 | tf_op jit(solution)/shard_map/all_to_all | solution.py:78
  1440.5 57.4 %reshape.435 = bf16[3072,1,4096]{2,1,0:T(2,128)(2,1)} reshape(bf16[8,2,786432]{2,1,0:T(2,128)(2,1)} %all-to-all-done.1) | data formatting | bytes 50331648
  1497.9 43.7 %copy.75 = bf16[1,3072,4096]{2,1,0:T(8,128)(2,1)} copy(bf16[1,3072,4096]{2,0,1:T(2,128)(2,1)} %bitcast.114) | data formatting | bytes 50331648
  1541.6 40.0 %gather_fusion.1 = bf16[2048,4096]{1,0:T(8,128)(2,1)} fusion(bf16[3072,4096]{1,0:T(8,128)(2,1)} %bitcast.112, s32[2048]{0:T(1024)S(1)} %copy-done.1), kind=kCustom, calls=%fused_computation.1 | custom fusion | bytes 33562624 | tf_op jit(solution)/shard_map/jit(_take)/gather | solution.py:79
  1581.6 27.2 %reshape.403 = bf16[1024,2,4096]{2,1,0:T(2,128)(2,1)} reshape(bf16[2048,4096]{1,0:T(8,128)(2,1)} %gather_fusion.1) | data formatting | bytes 33554432 | tf_op jit(solution)/shard_map/jit(_take)/gather | solution.py:79
  1608.9 64.2 %multiply_reduce_fusion = f32[1024,4096]{1,0:T(8,128)} fusion(bf16[1024,2,4096]{2,1,0:T(2,128)(2,1)} %reshape.403, pred[1024,2]{1,0:T(8,128)(4,1)S(1)} %copy-done.7, f32[1024,2]{1,0:T(8,128)S(1)} %fusion.47), kind=kLoop, calls=%fused_computation.5 | loop fusion | flops 29360128 | bytes 33564672 | tf_op jit(solution)/shard_map/reduce_sum | solution.py:80
  1673.1 17.8 %fusion.12 = bf16[1,1024,4096]{2,1,0:T(8,128)(2,1)} fusion(f32[1,1024,4096]{2,1,0:T(8,128)} %all-reduce.5.cloned.1.call-done, bf16[1,1024,4096]{2,1,0:T(8,128)(2,1)} %get-tuple-element.6, f32[1024,4096]{1,0:T(8,128)} %multiply_reduce_fusion), kind=kLoop, calls=%fused_computation.31 | loop fusion | flops 16777216 | bytes 50331648 | tf_op jit(solution)/shard_map/convert_element_type | solution.py:93
  (68 shorter events, 3.1 us)
Async XLA Ops:
  6.5 1256.5 %copy-start = (bf16[4096,8]{0,1:T(8,128)(2,1)S(1)}, bf16[4096,8]{0,1:T(8,128)(2,1)}, u32[]{:S(2)}) copy-start(bf16[4096,8]{0,1:T(8,128)(2,1)} %param.30) | copy-start | bytes 196612
  6.6 419.8 %all-reduce.3.cloned.1.call-start = ((), (), s32[]{:S(2)}) async-start(), calls=%async_computation.2 | async-start | bytes 33554432 | tf_op jit(solution)/shard_map/psum | solution.py:44
  37.6 13.0 copy-start.4
  37.6 27.2 %slice-start = ((s8[8388608]{0:T(1024)(128)(4,1)}), s8[4194304]{0:T(1024)(128)(4,1)S(1)}, s32[]{:S(2)}) async-start(s8[8388608]{0:T(1024)(128)(4,1)} %bitcast.116), calls=%async_computation.4 | async-start | bytes 8388608
  50.7 14.2 slice-start.1
  64.9 14.0 copy-start.5
  82.2 14.2 copy-start.6
  132.3 0.7 copy-start.13
  132.3 0.7 copy-start.8
  132.3 0.7 copy-start.10
  509.8 7.8 copy-start.14
  509.8 325.3 %slice-start.2 = ((s8[11272192]{0:T(1024)(128)(4,1)}), s8[2883584]{0:T(1024)(128)(4,1)S(1)}, s32[]{:S(2)}) async-start(s8[11272192]{0:T(1024)(128)(4,1)} %bitcast.123), calls=%async_computation.6 | async-start | bytes 5767168
  509.8 281.1 %all-to-all-start = ((bf16[8,384,4096]{2,1,0:T(8,128)(2,1)}), bf16[8,384,4096]{2,1,0:T(8,128)(2,1)}, u32[]{:S(2)}, u32[]{:S(2)}) async-start(bf16[8,384,4096]{2,1,0:T(8,128)(2,1)} %broadcast_select_fusion.1), calls=%async_computation | async-start | bytes 50331648 | tf_op jit(solution)/shard_map/all_to_all | solution.py:76
  790.9 44.2 %slice-start.3 = ((s8[11272192]{0:T(1024)(128)(4,1)}), s8[4194304]{0:T(1024)(128)(4,1)S(1)}, s32[]{:S(2)}) async-start(s8[11272192]{0:T(1024)(128)(4,1)} %bitcast.123), calls=%async_computation.7 | async-start | bytes 8388608
  790.9 44.2 %slice-start.4 = ((s8[11272192]{0:T(1024)(128)(4,1)}), s8[4194304]{0:T(1024)(128)(4,1)S(1)}, s32[]{:S(2)}) async-start(s8[11272192]{0:T(1024)(128)(4,1)} %bitcast.123), calls=%async_computation.8 | async-start | bytes 8388608
  1159.6 7.5 copy-start.12
  1159.6 7.5 copy-start.15
  1159.6 280.8 %all-to-all-start.1 = ((bf16[8,2,786432]{2,1,0:T(2,128)(2,1)}), bf16[8,2,786432]{2,1,0:T(2,128)(2,1)}, u32[]{:S(2)}, u32[]{:S(2)}) async-start(bf16[8,2,786432]{2,1,0:T(2,128)(2,1)} %reshape.434), calls=%async_computation.1 | async-start | bytes 50331648 | tf_op jit(solution)/shard_map/all_to_all | solution.py:78
  1167.1 506.0 %all-reduce.5.cloned.1.call-start = ((), (), s32[]{:S(2)}) async-start(), calls=%async_computation.3 | async-start | bytes 33554432 | tf_op jit(solution)/shard_map/psum | solution.py:51
  1259.4 0.7 copy-start.11
  1259.4 0.9 copy-start.9
  1260.3 2.7 copy-start.2
  1268.7 13.0 copy-start.3
  1497.9 43.7 %copy-start.1 = (s32[2048]{0:T(1024)S(1)}, s32[2048]{0:T(1024)}, u32[]{:S(2)}) copy-start(s32[2048]{0:T(1024)} %broadcast_clamp_fusion) | copy-start | bytes 24580
  1581.6 27.2 %copy-start.7 = (pred[1024,2]{1,0:T(8,128)(4,1)S(1)}, pred[1024,2]{1,0:T(8,128)(4,1)}, u32[]{:S(2)}) copy-start(pred[1024,2]{1,0:T(8,128)(4,1)} %compare_and_fusion) | copy-start | bytes 6148
Sparse Core Ops, SparseCore 0:
  132.4 293.8 all-reduce.2
  1259.6 289.7 all-reduce.4
where the time goes:
time: 1710 us; the launch traced here: 1700 us
  waiting for transfers between devices  714 us (42%)
  local copies, waits for them, and re-layouts  347 us (20%)
  matrix products  322 us (19%)
  other arithmetic  286 us (17%)
    psum x1, waiting for transfers between devices, dense_branch(): attn_sum = lax.psum(attn_part, 'tp')  284 us
    all_to_all x1, waiting for transfers between devices, moe_branch(): recv_buf = lax.all_to_all(send_buf, 'ep', 0, 1, tiled=True)  272 us
    all_to_all x1, waiting for transfers between devices, moe_branch(): lax.all_to_all(expert_out, 'ep', 1, 0, tiled=True)  158 us
    unnamed x3, other arithmetic  152 us
    unnamed x50, local copies, waits for them, and re-layouts  152 us
    gather x2, local copies, waits for them, and re-layouts, moe_branch(): per_copy = jnp.take(returned, flat_pos, axis=0)  67.3 us
    reduce_sum x1, other arithmetic, moe_branch(): moe_out = jnp.sum(gates[:, :, None] * per_copy.astype(jnp.float32), axis=1)  64.2 us
    convert_element_type x1, local copies, waits for them, and re-layouts, expert_swiglu(): jnp.einsum('erf,efd->erd', hidden_act, exp_down, preferred_element_type=j...  57.9 us
  transfers between devices with their start and end apart: 4, of which 3 were waited for; matrix products, arithmetic and copies ran while one was open for 21% of the time, Pallas kernels for 0%

commit v1 on v0

v1 whole, which is shorter than its diff:
```python
import functools

import jax
import jax.numpy as jnp
from jax import lax
from jax.experimental import pallas as pl
from jax.experimental.pallas import tpu as pltpu
from jax.sharding import PartitionSpec as P

EPS = 1e-6
ROPE_BASE = 10000.0
QBLK = 256
MESH = pl.DeviceIdType.MESH
F32, BF16 = jnp.float32, jnp.bfloat16


def rope_tables(seq_len, head_dim):
    inv_freq = ROPE_BASE ** (-jnp.arange(head_dim // 2, dtype=F32) * (2.0 / head_dim))
    angle = jnp.arange(seq_len, dtype=F32)[:, None] * inv_freq[None, :]
    cos, sin = jnp.cos(angle), jnp.sin(angle)
    return jnp.concatenate([cos, cos], axis=1), jnp.concatenate([-sin, sin], axis=1)


def attn_kernel(scale, cos_ref, sin_ref, q_ref, k_ref, v_ref, o_ref, kr_ref):
    half = q_ref.shape[2] // 2
    q_rows = q_ref.shape[1]

    def rope(val, cos, sin):
        return (val * cos + pltpu.roll(val, half, 1) * sin).astype(BF16)

    kr_ref[...] = rope(k_ref[0], cos_ref[...], sin_ref[...])
    for blk in range(q_rows // QBLK):
        base = blk * QBLK
        rows = pl.ds(base, QBLK)
        query = rope(q_ref[0, rows, :], cos_ref[rows, :], sin_ref[rows, :])

        def score(lo, hi):
            return lax.dot_general(query, kr_ref[lo:hi, :], (((1,), (1,)), ((), ())), preferred_element_type=F32)

        diag = score(base, base + QBLK)
        row = lax.broadcasted_iota(jnp.int32, diag.shape, 0)
        col = lax.broadcasted_iota(jnp.int32, diag.shape, 1)
        scores = jnp.where(row >= col, diag, -1e30)
        if blk:
            scores = jnp.concatenate([score(0, base), scores], axis=1)
        top = jnp.max(scores, axis=1, keepdims=True)
        prob = jnp.exp((scores - top) * scale)
        prob = (prob * (1.0 / jnp.sum(prob, axis=1, keepdims=True))).astype(BF16)
        o_ref[rows, :] = jnp.dot(prob, v_ref[0, :base + QBLK, :], preferred_element_type=F32).astype(BF16)


def attention(query, keys, values, cos, sin):
    heads, rows, head_dim = query.shape
    tab = pl.BlockSpec((rows, head_dim), lambda h: (0, 0))
    spec = pl.BlockSpec((1, rows, head_dim), lambda h: (h, 0, 0))
    return pl.pallas_call(
        functools.partial(attn_kernel, head_dim ** -0.5),
        grid=(heads,),
        in_specs=[tab, tab, spec, spec, spec],
        out_specs=pl.BlockSpec((rows, head_dim), lambda h: (0, h)),
        out_shape=jax.ShapeDtypeStruct((rows, heads * head_dim), BF16),
        scratch_shapes=[pltpu.VMEM((rows, head_dim), BF16)],
        cost_estimate=pl.CostEstimate(flops=16 * heads * rows * rows * head_dim, bytes_accessed=heads * head_dim * rows * 12, transcendentals=heads * rows * rows),
    )(cos, sin, query, keys, values)


TILE = 256
CHUNKS = 4
NT_SLOTS = 3
NN_SLOTS = 4


def layer_kernel(tp, ep, ctx, w_out, x, gain, wg, wu, wd, recv, eg, eu, ed, row_of, gates,
                 out, c_l, c_r, c_o, a_l, a_r, a_o, wx, back,
                 lhs, h, fbuf, r1, r2, ybuf, a_own, a_in, a_mine, out_q, sel, wb1, wb2, wb3,
                 send_sem, recv_sem, ysend, yrecv, wsend, wrecv, sem1, sem2, sem3, lsem, osem):
    seq, d_model = out.shape
    rows = seq // CHUNKS
    quarter = rows // tp
    width = d_model // tp
    slots_all = recv.shape[0]
    sub = slots_all // ep
    me = lax.axis_index('tp')
    my_e = lax.axis_index('ep')
    right, left, far = lax.rem(me + 1, tp), lax.rem(me + tp - 1, tp), lax.rem(me + 2, tp)

    barrier = pltpu.get_barrier_semaphore()
    for peer in (right, far, left):
        pl.semaphore_signal(barrier, inc=1, device_id={'tp': peer}, device_id_type=MESH)
    for k in range(1, ep):
        pl.semaphore_signal(barrier, inc=1, device_id={'ep': lax.rem(my_e + k, ep)}, device_id_type=MESH)
    pl.semaphore_wait(barrier, 3 + ep - 1)

    def at(start, size, align):
        return pl.ds(pl.multiple_of(start, align), size)

    def remote(kind, c, d, src, dst):
        return pltpu.make_async_remote_copy(
            src_ref=src, dst_ref=dst, send_sem=send_sem.at[kind, c, d], recv_sem=recv_sem.at[kind, c, d],
            device_id={'tp': (right, left)[d]}, device_id_type=MESH)

    half = rows // 2

    def c_first(c, d):
        piece = at(c * rows, rows, rows)
        return remote(0, c, d, ctx.at[piece, :], (c_l, c_r)[d].at[piece, :])

    def c_second(c, d):
        piece = at(c * rows + d * half, half, half)
        return remote(1, c, d, (c_l, c_r)[d].at[piece, :], c_o.at[piece, :])

    def a_first(c, d):
        piece = at(c * rows, rows, rows)
        return remote(2, c, d, a_own.at[piece, :], (a_l, a_r)[d].at[piece, :])

    def a_second(c, d):
        piece = at(c * rows + d * half, half, half)
        return remote(3, c, d, (a_l, a_r)[d].at[piece, :], a_o.at[piece, :])

    q_half = quarter // 2

    def r_first(c, d):
        return remote(4, c, d, fbuf.at[lax.rem(c, 2), at(far * quarter + d * q_half, q_half, q_half), :], r1.at[c, d])

    def r_second(c, d):
        return remote(5, c, d, fbuf.at[lax.rem(c, 2), at((right, left)[d] * quarter, quarter, quarter), :], r2.at[c, d])

    def o_first(c, d):
        return remote(6, c, d, out_q.at[c], out.at[at(c * rows + me * quarter, quarter, quarter), :])

    def o_second(c, d):
        piece = at(c * rows + (left, right)[d] * quarter + d * q_half, q_half, q_half)
        return remote(7, c, d, out.at[piece, :], out.at[piece, :])

    def start(make, c):
        make(c, 0).start()
        make(c, 1).start()

    def arrived(make, c):
        make(c, 0).wait_recv()
        make(c, 1).wait_recv()

    def sent(make, c):
        make(c, 0).wait_send()
        make(c, 1).wait_send()

    share = w_out.shape[0] // ep
    cores = 2
    chips = ep // cores

    def w_first(k):
        peer = lax.rem(me + k, tp)
        return pltpu.make_async_remote_copy(
            src_ref=w_out.at[at(my_e * share, share, share), at(peer * width, width, width)],
            dst_ref=wx.at[me, at(my_e * share, share, share), :],
            send_sem=wsend.at[0, 0, k], recv_sem=wrecv.at[0, 0, k], device_id={'tp': peer}, device_id_type=MESH)

    def w_piece(stage, m, k, owner, peer):
        piece = wx.at[lax.rem(me + tp - k, tp), at(owner * share, share, share), :]
        return pltpu.make_async_remote_copy(
            src_ref=piece, dst_ref=piece, send_sem=wsend.at[stage, m, k], recv_sem=wrecv.at[stage, m, k],
            device_id={'ep': peer}, device_id_type=MESH)

    def w_second(m, k):
        return w_piece(1, m, k, my_e, lax.rem(my_e + cores * m, ep))

    def w_third(m, k):
        return w_piece(2, m, k, lax.rem(my_e + ep - cores * m, ep), my_e + 1 - 2 * lax.rem(my_e, 2))

    def each(count, low, do):
        def outer(m, carry):
            def inner(k, carry):
                do(m, k)
                return carry
            return lax.fori_loop(1, tp, inner, carry)
        lax.fori_loop(low, count, outer, 0)

    def w_start():
        lax.fori_loop(1, tp, lambda k, carry: (w_first(k).start(), carry)[1], 0)

    def w_spread():
        lax.fori_loop(1, tp, lambda k, carry: (w_first(k).wait_recv(), carry)[1], 0)
        each(chips, 1, lambda m, k: w_second(m, k).start())
        each(1, 0, lambda m, k: w_third(m, k).start())

    def w_pair():
        def pass_on(m, k):
            w_second(m, k).wait_recv()
            w_third(m, k).start()
        each(chips, 1, pass_on)

    def w_done():
        each(chips, 0, lambda m, k: w_third(m, k).wait_recv())

    def w_sent():
        lax.fori_loop(1, tp, lambda k, carry: (w_first(k).wait_send(), carry)[1], 0)
        each(chips, 1, lambda m, k: w_second(m, k).wait_send())
        each(chips, 0, lambda m, k: w_third(m, k).wait_send())

    def gate_up(wa, wb, mid=None):
        total = wa.shape[0]
        full, tail = total // TILE, total % TILE

        def copies(i, slot, n):
            return [pltpu.make_async_copy(w.at[at(i * TILE, n, 32), :], wb1.at[slot, k, pl.ds(0, n), :], sem1.at[slot, k]) for k, w in enumerate((wa, wb))]

        def go(i, slot, n=TILE):
            for cp in copies(i, slot, n):
                cp.start()

        def ready(i, slot, n=TILE):
            for cp in copies(i, slot, n):
                cp.wait()

        def product(slot, n):
            dims = (((1,), (1,)), ((), ()))
            gate = lax.dot_general(lhs[...], wb1[slot, 0, :n, :], dims, preferred_element_type=F32)
            up = lax.dot_general(lhs[...], wb1[slot, 1, :n, :], dims, preferred_element_type=F32)
            return (jax.nn.silu(gate) * up).astype(BF16)

        ahead = NT_SLOTS - 1
        for j in range(ahead):
            go(j, j)

        def step(i, carry):
            nxt = i + ahead
            pl.when(nxt < full)(lambda: go(nxt, lax.rem(nxt, NT_SLOTS)))
            if tail:
                pl.when(nxt == full)(lambda: go(full, full % NT_SLOTS, tail))
            slot = lax.rem(i, NT_SLOTS)
            ready(i, slot)
            h[:, at(i * TILE, TILE, TILE)] = product(slot, TILE)
            if mid is not None:
                pl.when(i == full // 2)(mid)
            return carry

        lax.fori_loop(0, full, step, 0)
        if tail:
            ready(full, full % NT_SLOTS, tail)
            h[:, full * TILE:full * TILE + tail] = product(full % NT_SLOTS, tail)

    def columns(left_ref, depth, tiles, fetch, use):
        ahead = NN_SLOTS - 1

        def go(i, slot):
            for cp in fetch(i, slot):
                cp.start()

        for j in range(ahead):
            go(j, j)

        def step(i, carry):
            nxt = i + ahead
            pl.when(nxt < tiles)(lambda: go(nxt, lax.rem(nxt, NN_SLOTS)))
            slot = lax.rem(i, NN_SLOTS)
            for cp in fetch(i, slot):
                cp.wait()
            use(i, slot, jnp.dot(left_ref[:, :depth], wb2[slot, :depth, :], preferred_element_type=F32))
            return carry

        lax.fori_loop(0, tiles, step, 0)

    def whole_depth(w):
        def fetch(i, slot):
            return [pltpu.make_async_copy(w.at[:, at(i * TILE, TILE, TILE)], wb2.at[slot, pl.ds(0, w.shape[0]), :], sem2.at[slot, 0])]
        return fetch

    def set_off(c, carry):
        start(c_first, c)
        return carry

    def c_forward(c, carry):
        arrived(c_first, c)
        start(c_second, c)
        return carry

    def y_copy(e):
        return pltpu.make_async_remote_copy(
            src_ref=ybuf.at[pl.ds(e * sub, sub), :], dst_ref=back.at[at(my_e * sub, sub, sub), :],
            send_sem=ysend.at[e], recv_sem=yrecv.at[my_e], device_id={'ep': e}, device_id_type=MESH)

    def y_arrival(e):
        return pltpu.make_async_remote_copy(
            src_ref=ybuf.at[pl.ds(e * sub, sub), :], dst_ref=back.at[pl.ds(e * sub, sub), :],
            send_sem=ysend.at[e], recv_sem=yrecv.at[e], device_id={'ep': e}, device_id_type=MESH)

    def y_local(e):
        return pltpu.make_async_copy(ybuf.at[pl.ds(e * sub, sub), :], back.at[pl.ds(e * sub, sub), :], ysend.at[e])

    def expert(r, carry):
        load = pltpu.make_async_copy(recv.at[at(r * TILE, TILE, TILE), :], lhs, lsem.at[0])
        load.start()
        load.wait()
        gate_up(eg, eu)

        def keep(i, slot, acc):
            ybuf[at(r * TILE, TILE, TILE), at(i * TILE, TILE, TILE)] = acc.astype(BF16)
        columns(h, ed.shape[0], d_model // TILE, whole_depth(ed), keep)
        pl.when(r == 0)(w_spread)
        return carry
    w_start()
    lax.fori_loop(0, CHUNKS, set_off, 0)
    lax.fori_loop(0, slots_all // TILE, expert, 0)
    for e in range(ep):
        pl.when(e != my_e)(lambda e=e: y_copy(e).start())
        pl.when(e == my_e)(lambda e=e: y_local(e).start())
    w_pair()
    lax.fori_loop(0, CHUNKS, c_forward, 0)

    def project(c, carry):
        arrived(c_second, c)
        piece = at(c * rows, rows, rows)
        loads = [pltpu.make_async_copy(src.at[piece, :], lhs.at[:, at(who * width, width, width)], lsem.at[k])
                 for k, (src, who) in enumerate(((ctx, me), (c_r, right), (c_o, far), (c_l, left)))]
        loads.append(pltpu.make_async_copy(x.at[piece, at(me * width, width, width)], a_own.at[piece, :], lsem.at[4]))
        for cp in loads:
            cp.start()
        for cp in loads:
            cp.wait()

        def keep(i, slot, acc):
            block = (piece, at(i * TILE, TILE, TILE))
            a_own[block] = (a_own[block].astype(F32) + acc).astype(BF16)

        def fetch(i, slot):
            cols = at(i * TILE, TILE, TILE)
            own = pltpu.make_async_copy(w_out.at[:, at(me * width + i * TILE, TILE, TILE)], wb2.at[slot, at(me * width, width, width), :], sem2.at[slot, 0])
            rest = [pltpu.make_async_copy(wx.at[who, :, cols], wb2.at[slot, at(who * width, width, width), :], sem2.at[slot, k])
                    for k, who in ((1, right), (2, far), (3, left))]
            return [own] + rest
        pl.when(c == 0)(w_done)
        columns(lhs, d_model, width // TILE, fetch, keep)
        start(a_first, c)

        def forward():
            arrived(a_first, c - 1)
            start(a_second, c - 1)
        pl.when((c >= 1) & (c < CHUNKS - 1))(forward)
        return carry
    lax.fori_loop(0, CHUNKS, project, 0)

    def a_forward(c):
        arrived(a_first, c)
        start(a_second, c)

    def reduce_on(c):
        for d, who in ((0, right), (1, left)):
            r_first(c, d).wait_recv()

            def add(k, carry, d=d, who=who):
                block = (lax.rem(c, 2), at(who * quarter + d * q_half + k * 8, 8, 8), slice(None))
                fbuf[block] = fbuf[block] + r1[c, d, at(k * 8, 8, 8), :]
                return carry
            lax.fori_loop(0, q_half // 8, add, 0)
            r_second(c, d).start()

    def o_local(c):
        return pltpu.make_async_copy(out_q.at[c], out.at[at(c * rows + me * quarter, quarter, quarter), :], osem.at[c])

    def finish(c):
        arrived(r_second, c)

        def add(k, carry):
            part = at(k * 16, 16, 16)
            total = fbuf[lax.rem(c, 2), at(me * quarter + k * 16, 16, 16), :] + (r2[c, 0, part, :] + r2[c, 1, part, :])
            out_q[c, part, :] = (a_mine[c, part, :].astype(F32) + total).astype(BF16)
            return carry
        lax.fori_loop(0, quarter // 16, add, 0)
        start(o_first, c)
        o_local(c).start()

    def o_forward(c):
        arrived(o_first, c)
        start(o_second, c)

    def y_back():
        for e in range(ep):
            pl.when(e != my_e)(lambda e=e: y_arrival(e).wait_recv())
            pl.when(e == my_e)(lambda e=e: y_local(e).wait())

    def ffn(c, carry):
        arrived(a_second, c)
        piece = at(c * rows, rows, rows)
        loads = [pltpu.make_async_copy(src.at[piece, :], a_in.at[k], lsem.at[k]) for k, src in enumerate((a_r, a_o, a_l))]
        for cp in loads:
            cp.start()
        for cp in loads:
            cp.wait()
        parts = ((None, me), (0, right), (1, far), (2, left))

        def norm(k, carry):
            block = at(k * 16, 16, 16)
            vals = [(a_own[at(c * rows + k * 16, 16, 16), :] if p is None else a_in[p, block, :]).astype(F32) for p, _ in parts]
            square = sum(jnp.sum(v * v, axis=1, keepdims=True) for v in vals)
            inv = lax.rsqrt(square / d_model + EPS)
            for v, (_, who) in zip(vals, parts):
                cols = at(who * width, width, width)
                lhs[block, cols] = (v * inv * gain[:, cols]).astype(BF16)
            return carry
        lax.fori_loop(0, rows // 16, norm, 0)
        for p, who in parts:
            mine = at(me * quarter, quarter, quarter)
            val = a_own[at(c * rows + me * quarter, quarter, quarter), :] if p is None else a_in[p, mine, :]
            a_mine[c, :, at(who * width, width, width)] = val
        for j in range(row_of.shape[1]):
            target = row_of[piece, j:j + 1]
            sel[j * rows:(j + 1) * rows, :] = jnp.where(lax.broadcasted_iota(jnp.int32, (rows, slots_all), 1) == target, 1.0, 0.0).astype(BF16)

        def mid():
            pl.when(c == 0)(lambda: a_forward(CHUNKS - 2))
            pl.when(c >= 1)(lambda: reduce_on(c - 1))
        gate_up(wg, wu, mid)
        @pl.when(c == 0)
        def _():
            a_forward(CHUNKS - 1)
            y_back()

        @pl.when(c >= 2)
        def _():
            o_forward(c - 2)
            sent(r_first, c - 2)
            sent(r_second, c - 2)

        def keep(i, slot, acc):
            copies = jnp.dot(sel[...], wb3[slot], preferred_element_type=F32)
            for j in range(row_of.shape[1]):
                acc = acc + gates[piece, j:j + 1] * copies[j * rows:(j + 1) * rows]
            fbuf[lax.rem(c, 2), :, at(i * TILE, TILE, TILE)] = acc
        down = whole_depth(wd)

        def fetch(i, slot):
            return down(i, slot) + [pltpu.make_async_copy(back.at[:, at(i * TILE, TILE, TILE)], wb3.at[slot], sem3.at[slot])]
        columns(h, wd.shape[0], d_model // TILE, fetch, keep)
        start(r_first, c)
        pl.when(c >= 1)(lambda: finish(c - 1))
        return carry
    lax.fori_loop(0, CHUNKS, ffn, 0)
    reduce_on(CHUNKS - 1)
    o_forward(CHUNKS - 2)
    finish(CHUNKS - 1)
    o_forward(CHUNKS - 1)

    def drain(c, carry):
        arrived(o_second, c)
        o_local(c).wait()
        for make in (c_first, c_second, a_first, a_second, o_first, o_second):
            sent(make, c)

        @pl.when(c >= CHUNKS - 2)
        def _():
            sent(r_first, c)
            sent(r_second, c)
        return carry
    lax.fori_loop(0, CHUNKS, drain, 0)
    for e in range(ep):
        pl.when(e != my_e)(lambda e=e: y_copy(e).wait_send())
    w_sent()


def fused_layer(tp, ep, ctx, w_out, x, gain, wg, wu, wd, recv, eg, eu, ed, row_of, gates):
    seq, d_model = x.shape
    rows = seq // CHUNKS
    quarter = rows // tp
    width = d_model // tp
    hidden = wd.shape[0]
    slots_all = recv.shape[0]
    top_k = row_of.shape[1]
    any_spec = pl.BlockSpec(memory_space=pl.ANY)
    vmem_spec = pl.BlockSpec(memory_space=pltpu.VMEM)
    part = jax.ShapeDtypeStruct((seq, width), BF16)
    outs = pl.pallas_call(
        functools.partial(layer_kernel, tp, ep),
        out_shape=[jax.ShapeDtypeStruct((seq, d_model), BF16)] + [part] * 6 + [jax.ShapeDtypeStruct((tp, w_out.shape[0], width), BF16), jax.ShapeDtypeStruct((slots_all, d_model), BF16)],
        in_specs=[any_spec] * 3 + [vmem_spec] + [any_spec] * 7 + [vmem_spec] * 2,
        out_specs=[any_spec] * 9,
        scratch_shapes=[
            pltpu.VMEM((rows, d_model), BF16),
            pltpu.VMEM((rows, hidden), BF16),
            pltpu.VMEM((2, rows, d_model), F32),
            pltpu.VMEM((CHUNKS, 2, quarter // 2, d_model), F32),
            pltpu.VMEM((CHUNKS, 2, quarter, d_model), F32),
            pltpu.VMEM((slots_all, d_model), BF16),
            pltpu.VMEM((seq, width), BF16),
            pltpu.VMEM((3, rows, width), BF16),
            pltpu.VMEM((CHUNKS, quarter, d_model), BF16),
            pltpu.VMEM((CHUNKS, quarter, d_model), BF16),
            pltpu.VMEM((top_k * rows, slots_all), BF16),
            pltpu.VMEM((NT_SLOTS, 2, TILE, d_model), BF16),
            pltpu.VMEM((NN_SLOTS, d_model, TILE), BF16),
            pltpu.VMEM((NN_SLOTS, slots_all, TILE), BF16),
            pltpu.SemaphoreType.DMA((8, CHUNKS, 2)),
            pltpu.SemaphoreType.DMA((8, CHUNKS, 2)),
            pltpu.SemaphoreType.DMA((ep,)),
            pltpu.SemaphoreType.DMA((ep,)),
            pltpu.SemaphoreType.DMA((3, ep // 2, tp)),
            pltpu.SemaphoreType.DMA((3, ep // 2, tp)),
            pltpu.SemaphoreType.DMA((NT_SLOTS, 2)),
            pltpu.SemaphoreType.DMA((NN_SLOTS, 4)),
            pltpu.SemaphoreType.DMA((NN_SLOTS,)),
            pltpu.SemaphoreType.DMA((5,)),
            pltpu.SemaphoreType.DMA((CHUNKS,)),
        ],
        compiler_params=pltpu.CompilerParams(collective_id=0, has_side_effects=True, vmem_limit_bytes=67043328),
        cost_estimate=pl.CostEstimate(flops=6 * seq * d_model * hidden, bytes_accessed=300 * 2 ** 20, transcendentals=seq * hidden),
    )(ctx, w_out, x, gain, wg, wu, wd, recv, eg, eu, ed, row_of, gates)
    return outs[0]


def solution(mesh):
    tok_spec = P(('dp', 'ep'), None, None)
    col_spec = P(None, 'tp', None)
    exp_spec = P('ep', None, None)
    in_specs = (tok_spec, tok_spec, tok_spec, P(None), col_spec, col_spec, col_spec, P('tp', None, None), P(None), P(None, 'tp'), P(None, 'tp'), P('tp', None), P(None), P(None, None), exp_spec, exp_spec, exp_spec)
    tp = mesh.shape['tp']
    ep = mesh.shape['ep']

    def layer_local(hidden_in, expert_ids, slot_ids, attn_gain, w_query, w_key, w_value, w_out, ffn_gain, w_gate, w_up, w_down, moe_gain, w_router, exp_gate, exp_up, exp_down):
        _, seq, d_model = hidden_in.shape
        heads, head_dim = w_query.shape[1:]
        experts = w_router.shape[1]
        top_k = expert_ids.shape[2]
        cap = 3 * seq * top_k // (2 * experts)
        sub = cap // tp
        rank = lax.axis_index('tp')
        x = hidden_in[0]
        x_f32 = x.astype(F32)
        unit = x_f32 * lax.rsqrt(jnp.mean(x_f32 * x_f32, axis=-1, keepdims=True) + EPS)
        n = (unit * attn_gain.astype(F32)).astype(BF16)
        u = (unit * moe_gain.astype(F32)).astype(BF16)

        ids, slots = expert_ids[0], slot_ids[0]
        row_of = jnp.where(slots % tp == rank, ids * sub + slots // tp, -1)
        rows = lax.broadcasted_iota(jnp.int32, (experts * sub, seq), 0)
        pick = sum((rows == row_of[:, j][None, :]) for j in range(top_k)).astype(BF16)
        send = jnp.dot(pick, u, preferred_element_type=F32).astype(BF16).reshape(experts, sub, d_model)
        recv = lax.all_to_all(send, 'ep', 0, 0, tiled=True).reshape(experts * sub, d_model)
        logits = jnp.dot(u, w_router, preferred_element_type=F32)
        picked = [jnp.sum(jnp.where(lax.broadcasted_iota(jnp.int32, logits.shape, 1) == ids[:, j:j + 1], logits, 0.0), axis=1, keepdims=True) for j in range(top_k)]
        gates = jax.nn.softmax(jnp.concatenate(picked, axis=1), axis=-1)

        n, _ = lax.optimization_barrier((n, send))
        cos, sin = rope_tables(seq, head_dim)
        q = jnp.einsum('sd,dhe->hse', n, w_query, preferred_element_type=F32)
        k = jnp.einsum('sd,dhe->hse', n, w_key, preferred_element_type=F32)
        v = jnp.einsum('sd,dhe->hse', n, w_value, preferred_element_type=F32).astype(BF16)
        ctx = attention(q, k, v, cos, sin)
        out = fused_layer(tp, ep, ctx, w_out.reshape(heads * head_dim, d_model), x, ffn_gain.astype(F32)[None], w_gate.T, w_up.T, w_down, recv,
                          exp_gate[0].T, exp_up[0].T, exp_down[0], row_of, gates)
        return out[None]

    return jax.shard_map(layer_local, mesh=mesh, in_specs=in_specs, out_specs=tok_spec, check_vma=False)
```

time: 1710 us -> 492 us (0.29)
  waiting for transfers between devices: 714 us -> 0.01 us
  Pallas kernels: 0 us -> 388 us
  local copies, waits for them, and re-layouts: 347 us -> 10.4 us
  other arithmetic: 286 us -> 21.1 us
  matrix products: 322 us -> 57.8 us
    all_to_all x2 -> x1, waiting for transfers between devices: 430 us -> 0.01 us  [layer_local(): lax.all_to_all(send, 'ep', 0, 0, tiled=True).reshape(experts * sub, d_model)]
    pallas_call x0 -> x2, Pallas kernels: none -> 388 us  [the longest x1 366 us: fused_layer(): pl.pallas_call(functools.partial(layer_kernel, tp, ep), out_shape=[jax.Sh...]
    psum x2 -> x0, waiting for transfers between devices: 284 us -> none  [the longest x1 284 us: dense_branch(): attn_sum = lax.psum(attn_part, 'tp')]
    dot_general x10 -> x5, matrix products: 281 us -> 57.8 us  [the longest x1 15.1 us: layer_local(): k = jnp.einsum('sd,dhe->hse', n, w_key, preferred_element_type=F32)]
    unnamed x3 -> x1, other arithmetic: 152 us -> 0.01 us
    unnamed x50 -> x23, local copies, waits for them, and re-layouts: 152 us -> 9.15 us
    gather x7 -> x0, local copies, waits for them, and re-layouts: 127 us -> none  [the longest x2 67.3 us: moe_branch(): per_copy = jnp.take(returned, flat_pos, axis=0)]
    reduce_sum x4 -> x2, other arithmetic: 85.6 us -> 5.13 us  [the longest x1 5.1 us: layer_local(): jnp.mean(x_f32 * x_f32, axis=-1, keepdims=True) + EPS]
  transfers between devices with their start and end apart: 4 -> 1, of which waited for: 3 -> 0; matrix products, arithmetic and copies ran while one was open for 21% -> 13% of each run, Pallas kernels for 0% -> 4%
where the time goes in v1:
time: 492 us; the launch traced here: 485 us
  Pallas kernels  388 us (79%)
  matrix products  57.8 us (12%)
  other arithmetic  21.1 us (4%)
  local copies, waits for them, and re-layouts  10.4 us (2%)
  starting transfers between devices  7.12 us (1%)
    pallas_call x1, Pallas kernels, fused_layer(): pl.pallas_call(functools.partial(layer_kernel, tp, ep), out_shape=[jax.Sh...  366 us
    pallas_call x1, Pallas kernels, attention(): pl.pallas_call(functools.partial(attn_kernel, head_dim ** (-0.5)), grid=(...  21.6 us
    dot_general x1, matrix products, layer_local(): k = jnp.einsum('sd,dhe->hse', n, w_key, preferred_element_type=F32)  15.1 us
    dot_general x1, matrix products, layer_local(): q = jnp.einsum('sd,dhe->hse', n, w_query, preferred_element_type=F32)  14.1 us
    dot_general x1, matrix products, layer_local(): jnp.dot(pick, u, preferred_element_type=F32).astype(BF16)  12.8 us
    convert_element_type x2, other arithmetic, layer_local(): n = (unit * attn_gain.astype(F32)).astype(BF16)  10.5 us
    dot_general x1, matrix products, layer_local(): jnp.einsum('sd,dhe->hse', n, w_value, preferred_element_type=F32)  10.1 us
  transfers between devices with their start and end apart: 1, of which 0 were waited for; matrix products, arithmetic and copies ran while one was open for 13% of the time, Pallas kernels for 4%

profile of v1, /device:TPU:97, one launch (start us, length us, event | category | flops | bytes accessed | tf_op | source)
XLA Modules:
  0.0 484.8 jit_solution(9524418677311029892)
XLA Ops:
  0.0 0.0 copy-start.4
  0.0 0.0 copy-start.2
  0.0 0.0 copy-start.3
  0.0 5.1 %fusion.4 = f32[1024]{0:T(1024)S(1)} fusion(bf16[1,1024,4096]{2,1,0:T(8,128)(2,1)} %param.17), kind=kLoop, calls=%fused_computation.6 | loop fusion | flops 12581888 | bytes 8392704 | tf_op jit(solution)/shard_map/reduce_sum | solution.py:527
  5.1 0.0 copy-done.4
  5.2 0.0 copy-done.2
  5.2 0.2 copy.38
  5.4 0.0 copy-done.3
  5.4 0.2 copy.37
  5.6 0.5 fusion.35.row_of
  6.1 0.0 copy-start.1
  6.2 0.8 copy-done.1
  7.0 0.5 slice_reduce_fusion.3
  7.5 12.8 %convolution_convert_fusion = bf16[768,4096]{1,0:T(8,128)(2,1)} fusion(f32[4096]{0:T(1024)S(1)} %convert_element_type.39, f32[1024]{0:T(1024)S(1)} %add_rsqrt_fusion, s32[1024]{0:T(1024)S(1)} %get-tuple-element.12, s32[1024]{0:T(1024)S(1)} %get-tuple-element.11, bf16[1,1024,4096]{2,1,0:T(8,128)(2,1)} %param.17), kind=kOutput, calls=%fused_computation.16 | convolution fusion | flops 6467092480 | bytes 14708736 | tf_op jit(solution)/shard_map/dot_general | solution.py:535
  20.3 0.0 copy-start.5
  20.3 0.0 copy-start.6
  20.3 0.0 copy-start.7
  20.3 7.1 %all-to-all-start = ((bf16[8,96,4096]{2,1,0:T(8,128)(2,1)}), bf16[8,96,4096]{2,1,0:T(8,128)(2,1)}, u32[]{:S(2)}, u32[]{:S(2)}) async-start(bf16[8,96,4096]{2,1,0:T(8,128)(2,1)} %bitcast.70), calls=%async_computation | async-start | bytes 12582912 | tf_op jit(solution)/shard_map/all_to_all | solution.py:536
  27.4 0.0 copy-done.5
  27.5 0.0 copy-done.6
  27.5 0.6 broadcast_in_dim.34
  28.1 0.5 slice_reduce_fusion.1
  28.6 0.0 copy-done.7
  28.6 5.7 %select_reduce_fusion.1 = (f32[1024]{0:T(1024)S(1)}, f32[1024]{0:T(1024)S(1)}) fusion(s32[1024]{0:T(1024)S(1)} %get-tuple-element.9, s32[1024]{0:T(1024)S(1)} %get-tuple-element.10, bf16[4096,8]{0,1:T(8,128)(2,1)S(1)} %copy-done.7, f32[4096]{0:T(1024)S(1)} %convert_element_type.39, f32[1024]{0:T(1024)S(1)} %add_rsqrt_fusion, bf16[1,1024,4096]{2,1,0:T(8,128)(2,1)} %param.17), kind=kOutput, calls=%fused_computation.52 | convolution fusion | flops 83933184 | bytes 8491008 | tf_op jit(solution)/shard_map/dot_general | solution.py:537
  34.4 0.2 copy.42
  34.6 2.0 fusion.41
  36.6 10.5 %fusion.2 = bf16[1024,4096]{1,0:T(8,128)(2,1)} fusion(f32[4096]{0:T(1024)S(1)} %convert_element_type.34, f32[1024]{0:T(1024)S(1)} %add_rsqrt_fusion, bf16[1,1024,4096]{2,1,0:T(8,128)(2,1)} %param.17), kind=kLoop, calls=%fused_computation.4 | loop fusion | flops 16777216 | bytes 16797696 | tf_op jit(solution)/shard_map/convert_element_type | solution.py:528
  47.1 0.0 copy-start
  47.1 0.0 slice-start
  47.1 15.1 %fusion.22.k_ref = f32[8,1024,128]{2,1,0:T(8,128)} fusion(bf16[4096,8,128]{2,1,0:T(8,128)(2,1)} %param.22, bf16[1024,4096]{1,0:T(8,128)(2,1)} %fusion.2), kind=kOutput, calls=%fused_computation.22 | convolution fusion | flops 8589934592 | bytes 20971520 | tf_op jit(solution)/shard_map/sd,dhe->hse/dot_general | solution.py:544
  62.2 0.0 copy-done
  62.2 0.0 slice-start.1
  62.2 14.1 %fusion.17.q_ref = f32[8,1024,128]{2,1,0:T(8,128)} fusion(bf16[4096,8,128]{2,1,0:T(8,128)(2,1)} %param.21, bf16[1024,4096]{1,0:T(8,128)(2,1)S(1)} %copy-done), kind=kOutput, calls=%fused_computation.21 | convolution fusion | flops 8589934592 | bytes 20971520 | tf_op jit(solution)/shard_map/sd,dhe->hse/dot_general | solution.py:543
  76.3 1.0 broadcast_divide_fusion.gates
  77.3 1.4 pad_maximum_fusion
  78.7 0.0 slice-done
  78.7 0.0 slice-done.1
  78.7 10.1 %convert_bitcast_fusion.v_ref = bf16[8,1024,128]{2,1,0:T(8,128)(2,1)} fusion(bf16[4096,8,128]{2,1,0:T(8,128)(2,1)S(1)} %bitcast.80, bf16[1024,4096]{1,0:T(8,128)(2,1)S(1)} %copy-done), kind=kOutput, calls=%fused_computation.23 | convolution fusion | flops 8590983168 | bytes 18874368 | tf_op jit(solution)/shard_map/sd,dhe->hse/dot_general | solution.py:545
  88.7 21.6 %shard_map.163.ctx = bf16[1024,1024]{1,0:T(8,128)(2,1)} custom-call(f32[1024,128]{1,0:T(8,128)} %get-tuple-element.20.cos_ref, f32[1024,128]{1,0:T(8,128)} %get-tuple-element.21.sin_ref, f32[8,1024,128]{2,1,0:T(8,128)} %fusion.17.q_ref, f32[8,1024,128]{2,1,0:T(8,128)} %fusion.22.k_ref, bf16[8,1024,128]{2,1,0:T(8,128)(2,1)} %convert_bitcast_fusion.v_ref), custom_call_target="tpu_custom_call" | custom-call | flops 17179869184 | bytes 12582912 | tf_op jit(solution)/shard_map/pallas_call | solution.py:56
  110.3 0.0 all-to-all-done
  110.3 366.1 %shard_map.164 = (bf16[1024,4096]{1,0:T(8,128)(2,1)}, bf16[1024,1024]{1,0:T(8,128)(2,1)}, bf16[1024,1024]{1,0:T(8,128)(2,1)}, bf16[1024,1024]{1,0:T(8,128)(2,1)}...) custom-call(bf16[1024,1024]{1,0:T(8,128)(2,1)} %shard_map.163.ctx, ...), custom_call_target="tpu_custom_call" | custom-call | flops 69256347648 | bytes 314572800 | tf_op jit(solution)/shard_map/pallas_call | solution.py:471
  476.4 7.9 %copy.56 = bf16[1,1024,4096]{2,1,0:T(8,128)(2,1)} copy(bf16[1,1024,4096]{2,1,0:T(8,128)(2,1)} %bitcast.68) | data formatting | bytes 16777216
  (7 shorter events, 0.1 us)
Async XLA Ops:
  0.0 5.1 %copy-start.4 = (bf16[4096]{0:T(1024)(128)(2,1)S(1)}, bf16[4096]{0:T(1024)(128)(2,1)}, u32[]{:S(2)}) copy-start(bf16[4096]{0:T(1024)(128)(2,1)} %param.29) | copy-start | bytes 24580
  0.0 5.2 %copy-start.2 = (s32[1,1024,2]{1,2,0:T(2,128)S(1)}, s32[1,1024,2]{1,2,0:T(2,128)}, u32[]{:S(2)}) copy-start(s32[1,1024,2]{1,2,0:T(2,128)} %param.18) | copy-start | bytes 24580
  0.0 5.4 %copy-start.3 = (s32[1,1024,2]{1,2,0:T(2,128)S(1)}, s32[1,1024,2]{1,2,0:T(2,128)}, u32[]{:S(2)}) copy-start(s32[1,1024,2]{1,2,0:T(2,128)} %param.19) | copy-start | bytes 24580
  6.1 0.8 copy-start.1
  20.3 7.1 %copy-start.5 = (bf16[4096]{0:T(1024)(128)(2,1)S(1)}, bf16[4096]{0:T(1024)(128)(2,1)}, u32[]{:S(2)}) copy-start(bf16[4096]{0:T(1024)(128)(2,1)} %param.20) | copy-start | bytes 24580
  20.3 7.2 %copy-start.6 = (bf16[4096]{0:T(1024)(128)(2,1)S(1)}, bf16[4096]{0:T(1024)(128)(2,1)}, u32[]{:S(2)}) copy-start(bf16[4096]{0:T(1024)(128)(2,1)} %param.25) | copy-start | bytes 24580
  20.3 8.3 %copy-start.7 = (bf16[4096,8]{0,1:T(8,128)(2,1)S(1)}, bf16[4096,8]{0,1:T(8,128)(2,1)}, u32[]{:S(2)}) copy-start(bf16[4096,8]{0,1:T(8,128)(2,1)} %param.30) | copy-start | bytes 196612
  20.3 90.0 %all-to-all-start = ((bf16[8,96,4096]{2,1,0:T(8,128)(2,1)}), bf16[8,96,4096]{2,1,0:T(8,128)(2,1)}, u32[]{:S(2)}, u32[]{:S(2)}) async-start(bf16[8,96,4096]{2,1,0:T(8,128)(2,1)} %bitcast.70), calls=%async_computation | async-start | bytes 12582912 | tf_op jit(solution)/shard_map/all_to_all | solution.py:536
  47.1 15.1 %copy-start = (bf16[1024,4096]{1,0:T(8,128)(2,1)S(1)}, bf16[1024,4096]{1,0:T(8,128)(2,1)}, u32[]{:S(2)}) copy-start(bf16[1024,4096]{1,0:T(8,128)(2,1)} %fusion.2) | copy-start | bytes 25165828
  47.1 31.6 %slice-start = ((s8[8388608]{0:T(1024)(128)(4,1)}), s8[4194304]{0:T(1024)(128)(4,1)S(1)}, s32[]{:S(2)}) async-start(s8[8388608]{0:T(1024)(128)(4,1)} %bitcast.79), calls=%async_computation.1 | async-start | bytes 8388608
  62.2 16.5 %slice-start.1 = ((s8[8388608]{0:T(1024)(128)(4,1)}), s8[4194304]{0:T(1024)(128)(4,1)S(1)}, s32[]{:S(2)}) async-start(s8[8388608]{0:T(1024)(128)(4,1)} %bitcast.79), calls=%async_computation.2 | async-start | bytes 8388608

commit v2 on v0

v2 whole, which is shorter than its diff:
```python
import functools

import jax
import jax.numpy as jnp
import numpy as np
from jax import lax
from jax.experimental import pallas as pl
from jax.experimental.pallas import tpu as pltpu
from jax.sharding import PartitionSpec as P

EPS = 1e-6
ROPE_BASE = 10000.0
LOG2E = 1.4426950408889634
MESH = pl.DeviceIdType.MESH
F32, BF16 = jnp.float32, jnp.bfloat16


def rope_tables(seq_len, head_dim):
    inv_freq = np.float32(ROPE_BASE) ** (-np.arange(head_dim // 2, dtype=np.float32) * np.float32(2.0 / head_dim))
    angle = np.arange(seq_len, dtype=np.float32)[:, None] * inv_freq[None, :]
    cos, sin = np.cos(angle), np.sin(angle)
    return np.concatenate([cos, cos], axis=1), np.concatenate([-sin, sin], axis=1)


def prep_kernel(tp, blocks, x_ref, gain_ref, wr_ref, ids_ref, slots_ref, n_ref, route_ref, send_ref, u_ref, pick_ref):
    step = pl.program_id(0)
    size, cols = x_ref.shape[0], send_ref.shape[1]
    top_k = ids_ref.shape[0]
    slots_all = send_ref.shape[0]
    sub = slots_all // wr_ref.shape[0]

    @pl.when(step < blocks)
    def _():
        x = x_ref[...].astype(F32)
        unit = x * lax.rsqrt(jnp.mean(x * x, axis=-1, keepdims=True) + EPS)
        n_ref[...] = (unit * gain_ref[0:1, :]).astype(BF16)
        u = (unit * gain_ref[1:2, :]).astype(BF16)
        mine = pl.ds(pl.multiple_of(step * size, size), size)
        u_ref[mine, :] = u
        logits = lax.dot_general(wr_ref[...], u, (((1,), (1,)), ((), ())), preferred_element_type=F32)
        expert = lax.broadcasted_iota(jnp.int32, logits.shape, 0)
        picked = [jnp.sum(jnp.where(expert == ids_ref[j:j + 1, mine], logits, 0.0), axis=0, keepdims=True) for j in range(top_k)]
        top = functools.reduce(jnp.maximum, picked)
        weights = [jnp.exp(p - top) for p in picked]
        total = sum(weights)
        for j in range(top_k):
            route_ref[top_k + j:top_k + j + 1, mine] = weights[j] / total

    @pl.when(step == blocks)
    def _():
        rank = lax.axis_index('tp')
        rows = lax.broadcasted_iota(jnp.int32, pick_ref.shape, 0)
        hit = None
        for j in range(top_k):
            slot = slots_ref[j:j + 1, :]
            row_of = jnp.where(lax.rem(slot, tp) == rank, ids_ref[j:j + 1, :] * sub + lax.div(slot, tp), -1)
            route_ref[j:j + 1, :] = row_of.astype(F32)
            match = rows == row_of
            hit = match if hit is None else hit | match
        pick_ref[...] = jnp.where(hit, 1.0, 0.0).astype(BF16)

    @pl.when(step >= blocks)
    def _():
        part = pl.ds(pl.multiple_of((step - blocks) * cols, cols), cols)
        send_ref[...] = jnp.dot(pick_ref[...], u_ref[:, part], preferred_element_type=F32).astype(BF16)


def prepare(tp, x, gains, router, ids, slots, slots_all):
    seq, d_model = x.shape
    size, cols = 256, 512
    blocks, parts = seq // size, d_model // cols
    token = lambda i: (jnp.minimum(i, blocks - 1), 0)
    fixed = lambda i: (0, 0)
    return pl.pallas_call(
        functools.partial(prep_kernel, tp, blocks),
        grid=(blocks + parts,),
        in_specs=[pl.BlockSpec((size, d_model), token), pl.BlockSpec(gains.shape, fixed), pl.BlockSpec(router.shape, fixed),
                  pl.BlockSpec(ids.shape, fixed), pl.BlockSpec(slots.shape, fixed)],
        out_specs=[pl.BlockSpec((size, d_model), token), pl.BlockSpec((8, seq), fixed),
                   pl.BlockSpec((slots_all, cols), lambda i: (0, jnp.maximum(i - blocks, 0)))],
        out_shape=[jax.ShapeDtypeStruct((seq, d_model), BF16), jax.ShapeDtypeStruct((8, seq), F32), jax.ShapeDtypeStruct((slots_all, d_model), BF16)],
        scratch_shapes=[pltpu.VMEM((seq, d_model), BF16), pltpu.VMEM((slots_all, seq), BF16)],
        cost_estimate=pl.CostEstimate(flops=2 * slots_all * seq * d_model, bytes_accessed=6 * seq * d_model, transcendentals=0),
    )(x, gains, router, ids, slots)


def relay_kernel(heads, *refs):
    sources, o_ref = refs[:-1], refs[-1]
    depth, head_dim = o_ref.shape[0], sources[0].shape[1]
    block = 256
    span = block // heads
    row = lax.broadcasted_iota(jnp.int32, (block, block), 0)
    col = lax.broadcasted_iota(jnp.int32, (block, block), 1)
    order = jnp.where(col == (row % span) * heads + row // span, 1.0, 0.0).astype(BF16)
    for g in range(depth // span):
        for w, ref in enumerate(sources):
            moved = jnp.dot(order, ref[g * block:(g + 1) * block, :], preferred_element_type=F32).astype(BF16)
            for k in range(heads):
                lane = (w * heads + k) * head_dim
                o_ref[g * span:(g + 1) * span, lane:lane + head_dim] = moved[k * span:(k + 1) * span]


TILE = 256
CHUNKS = 4
PAIRS = 2
E_BLOCKS = 2
NT_SLOTS = 3
NN_SLOTS = 4


def layer_kernel(tp, ep, heads, top_k, n, wq, wk, wv, w_out, x, gain, wg, wu, wd, send, eg, eu, ed, route, cos_ref, sin_ref,
                 out, wqkv, c_l, c_r, c_o, a_l, a_r, a_o, wx, recv, y, back,
                 r1, r2, a_own, a_mine, out_q, wb1, wb2, wb3,
                 send_sem, recv_sem, dsend, drecv, ysend, yrecv, ysem, wsend, wrecv, sem1, sem2, sem3, lsem, osem):
    seq, d_model = out.shape
    rows = seq // CHUNKS
    quarter = rows // tp
    width = d_model // tp
    slots_all = recv.shape[0]
    sub = slots_all // ep
    me = lax.axis_index('tp')
    my_e = lax.axis_index('ep')
    right, left, far = lax.rem(me + 1, tp), lax.rem(me + tp - 1, tp), lax.rem(me + 2, tp)

    barrier = pltpu.get_barrier_semaphore()
    for peer in (right, far, left):
        pl.semaphore_signal(barrier, inc=1, device_id={'tp': peer}, device_id_type=MESH)
    for k in range(1, ep):
        pl.semaphore_signal(barrier, inc=1, device_id={'ep': lax.rem(my_e + k, ep)}, device_id_type=MESH)
    pl.semaphore_wait(barrier, 3 + ep - 1)

    def at(start, size, align):
        return pl.ds(pl.multiple_of(start, align), size)

    held = {}

    def remote(kind, c, d, src, dst):
        return pltpu.make_async_remote_copy(
            src_ref=src, dst_ref=dst, send_sem=send_sem.at[kind, c, d], recv_sem=recv_sem.at[kind, c, d],
            device_id={'tp': (right, left)[d]}, device_id_type=MESH)

    half = rows // 2

    def c_first(c, d):
        piece = at(c * rows, rows, rows)
        return remote(0, c, d, held['qkv'].at[piece, pl.ds(0, width)], (c_l, c_r)[d].at[piece, :])

    def c_second(c, d):
        piece = at(c * rows + d * half, half, half)
        return remote(1, c, d, (c_l, c_r)[d].at[piece, :], c_o.at[piece, :])

    def a_first(c, d):
        piece = at(c * rows, rows, rows)
        return remote(2, c, d, a_own.at[piece, :], (a_l, a_r)[d].at[piece, :])

    def a_second(c, d):
        piece = at(c * rows + d * half, half, half)
        return remote(3, c, d, (a_l, a_r)[d].at[piece, :], a_o.at[piece, :])

    q_half = quarter // 2

    def r_first(c, d):
        return remote(4, c, d, held['fbuf'].at[lax.rem(c, 2), at(far * quarter + d * q_half, q_half, q_half), :], r1.at[lax.rem(c, 2), d])

    def r_second(c, d):
        return remote(5, c, d, held['fbuf'].at[lax.rem(c, 2), at((right, left)[d] * quarter, quarter, quarter), :], r2.at[lax.rem(c, 2), d])

    def o_first(c, d):
        return remote(6, c, d, out_q.at[c], out.at[at(c * rows + me * quarter, quarter, quarter), :])

    def o_second(c, d):
        piece = at(c * rows + (left, right)[d] * quarter + d * q_half, q_half, q_half)
        return remote(7, c, d, out.at[piece, :], out.at[piece, :])

    def start(make, c):
        make(c, 0).start()
        make(c, 1).start()

    def arrived(make, c):
        make(c, 0).wait_recv()
        make(c, 1).wait_recv()

    def sent(make, c):
        make(c, 0).wait_send()
        make(c, 1).wait_send()

    share = w_out.shape[0] // 2
    core = lax.rem(my_e, 2)
    core_rows = at(core * share, share, share)

    def w_first(k):
        peer = lax.rem(me + k, tp)
        return pltpu.make_async_remote_copy(
            src_ref=w_out.at[core_rows, at(peer * width, width, width)], dst_ref=wx.at[me, core_rows, :],
            send_sem=wsend.at[0, k], recv_sem=wrecv.at[0, k], device_id={'tp': peer}, device_id_type=MESH)

    def w_second(k):
        piece = wx.at[lax.rem(me + tp - k, tp), core_rows, :]
        return pltpu.make_async_remote_copy(
            src_ref=piece, dst_ref=piece, send_sem=wsend.at[1, k], recv_sem=wrecv.at[1, k],
            device_id={'ep': my_e + 1 - 2 * core}, device_id_type=MESH)

    def w_start():
        for k in range(1, tp):
            w_first(k).start()

    def w_pair():
        for k in range(1, tp):
            w_first(k).wait_recv()
            w_second(k).start()

    def w_done():
        for k in range(1, tp):
            w_second(k).wait_recv()

    def w_sent():
        for k in range(1, tp):
            w_first(k).wait_send()
            w_second(k).wait_send()

    class Pair:
        def __init__(self, wa, wb):
            self.refs = (wa, wb)
            self.full, self.tail = wa.shape[0] // TILE, wa.shape[0] % TILE
            self.tiles = self.full + (self.tail > 0)

        def copies(self, i, slot, n=TILE):
            return [pltpu.make_async_copy(w.at[at(i * TILE, n, 32), :], wb1.at[slot, k, pl.ds(0, n), :], sem1.at[slot, k]) for k, w in enumerate(self.refs)]

        def go(self, i, slot, n=TILE):
            for cp in self.copies(i, slot, n):
                cp.start()

        def ready(self, i, slot, n=TILE):
            for cp in self.copies(i, slot, n):
                cp.wait()

    nt_ahead = NT_SLOTS - 1

    def gate_up(lhs, h, pair, base, then, mid=None):
        full, tail = pair.full, pair.tail

        def product(slot, n):
            dims = (((1,), (1,)), ((), ()))
            gate = lax.dot_general(lhs[:h.shape[0], :], wb1[slot, 0, :n, :], dims, preferred_element_type=F32)
            up = lax.dot_general(lhs[:h.shape[0], :], wb1[slot, 1, :n, :], dims, preferred_element_type=F32)
            return (jax.nn.silu(gate) * up).astype(BF16)

        def step(i, carry):
            nxt = i + nt_ahead
            ahead = lax.rem(base + nxt, NT_SLOTS)
            pl.when(nxt < full)(lambda: pair.go(nxt, ahead))
            if tail:
                pl.when(nxt == full)(lambda: pair.go(full, ahead, tail))
            pl.when(nxt >= pair.tiles)(lambda: then(nxt - pair.tiles, ahead))
            slot = lax.rem(base + i, NT_SLOTS)
            pair.ready(i, slot)
            h[:, at(i * TILE, TILE, TILE)] = product(slot, TILE)
            if mid is not None:
                pl.when(i == full // 2)(mid)
            return carry

        lax.fori_loop(0, full, step, 0)
        if tail:
            then(full + nt_ahead - pair.tiles, lax.rem(base + full + nt_ahead, NT_SLOTS))
            slot = lax.rem(base + full, NT_SLOTS)
            pair.ready(full, slot, tail)
            h[:, full * TILE:full * TILE + tail] = product(slot, tail)

    nn_ahead = NN_SLOTS - 1

    def go(fetch, i, slot):
        for cp in fetch(i, slot):
            cp.start()

    def prime(fetch):
        for j in range(nn_ahead):
            go(fetch, j, j)

    def columns(left_ref, m, depth, tiles, fetch, use, then=None):
        def step(i, carry):
            nxt = i + nn_ahead
            ahead = lax.rem(nxt, NN_SLOTS)
            pl.when(nxt < tiles)(lambda: go(fetch, nxt, ahead))
            if then is not None:
                pl.when(nxt >= tiles)(lambda: then(nxt - tiles, ahead))
            slot = lax.rem(i, NN_SLOTS)
            for cp in fetch(i, slot):
                cp.wait()
            use(i, slot, jnp.dot(left_ref[:m, :depth], wb2[slot, :depth, :], preferred_element_type=F32))
            return carry

        lax.fori_loop(0, tiles, step, 0)

    def whole_depth(w):
        def fetch(i, slot):
            return [pltpu.make_async_copy(w.at[:, at(i * TILE, TILE, TILE)], wb2.at[slot, pl.ds(0, w.shape[0]), :], sem2.at[slot, 0])]
        return fetch

    experts_in = Pair(eg, eu)
    ffn_in = Pair(wg, wu)
    from_qkv, from_ed, from_wd = whole_depth(wqkv), whole_depth(ed), whole_depth(wd)

    def from_out(i, slot):
        cols = at(i * TILE, TILE, TILE)
        own = pltpu.make_async_copy(w_out.at[:, at(me * width + i * TILE, TILE, TILE)], wb2.at[slot, at(me * width, width, width), :], sem2.at[slot, 0])
        rest = [pltpu.make_async_copy(wx.at[who, :, cols], wb2.at[slot, at(who * width, width, width), :], sem2.at[slot, k])
                for k, who in ((1, right), (2, far), (3, left))]
        return [own] + rest

    pair_rows = seq // PAIRS
    e_rows = slots_all // E_BLOCKS

    def c_forward(c):
        arrived(c_first, c)
        start(c_second, c)

    def d_copy(k):
        peer = lax.rem(my_e + k, ep)
        return pltpu.make_async_remote_copy(
            src_ref=send.at[at(peer * sub, sub, sub), :], dst_ref=recv.at[pl.ds((ep - k) * sub, sub), :],
            send_sem=dsend.at[k], recv_sem=drecv.at[k], device_id={'ep': peer}, device_id_type=MESH)

    own_rows = at(my_e * sub, sub, sub)
    d_local = pltpu.make_async_copy(send.at[own_rows, :], recv.at[pl.ds(0, sub), :], dsend.at[0])

    def y_copy(k):
        return pltpu.make_async_remote_copy(
            src_ref=y.at[pl.ds(k * sub, sub), :], dst_ref=back.at[own_rows, :],
            send_sem=ysend.at[k], recv_sem=yrecv.at[k], device_id={'ep': lax.rem(my_e + k, ep)}, device_id_type=MESH)

    y_local = pltpu.make_async_copy(y.at[pl.ds(0, sub), :], back.at[own_rows, :], ysend.at[0])

    def y_back():
        for k in range(1, ep):
            y_copy(k).wait_recv()
        y_local.wait()

    def a_forward(c):
        arrived(a_first, c)
        start(a_second, c)

    w_start()
    for k in range(1, ep):
        d_copy(k).start()
    d_local.start()

    head_dim = width // heads
    low = head_dim // 2

    def first_half(lhs, he, qkv, ystage):
        held['qkv'] = qkv

        def n_load(p):
            return pltpu.make_async_copy(n.at[pl.ds(p * pair_rows, pair_rows), :], lhs.at[pl.ds(0, pair_rows), :], lsem.at[0])

        def project_in(p, between=None):
            piece = pl.ds(p * pair_rows, pair_rows)
            n_load(p).wait()

            def rotate(val):
                parts = []
                for k in range(TILE // head_dim):
                    one = val[:, k * head_dim:(k + 1) * head_dim]
                    parts.append(one * cos_ref[piece, :] + pltpu.roll(one, low, 1) * sin_ref[piece, :])
                return jnp.concatenate(parts, axis=1)

            def keep(i, slot, acc):
                acc = jnp.where(i < 2 * width // TILE, rotate(acc), acc)
                qkv[piece, at(i * TILE, TILE, TILE)] = acc.astype(BF16)
            follow = from_qkv if p < PAIRS - 1 else from_out

            def then(i, slot):
                if between is not None:
                    pl.when(i == 0)(between)
                go(follow, i, slot)
            columns(lhs, pair_rows, d_model, 3 * width // TILE, from_qkv, keep, then)
            if p < PAIRS - 1:
                n_load(p + 1).start()

        def attend(c):
            base = c * rows
            keys = base + rows
            dims = (((1,), (1,)), ((), ()))

            def two(g, carry):
                for k in range(2):
                    hh = 2 * g + k
                    lane = lambda off: at(off + hh * head_dim, head_dim, head_dim)
                    query = qkv[base:keys, lane(0)]
                    scores = lax.dot_general(query, qkv[base:keys, lane(width)], dims, preferred_element_type=F32)
                    row = lax.broadcasted_iota(jnp.int32, scores.shape, 0)
                    col = lax.broadcasted_iota(jnp.int32, scores.shape, 1)
                    scores = jnp.where(row >= col, scores, -1e30)
                    if c:
                        before = lax.dot_general(query, qkv[0:base, lane(width)], dims, preferred_element_type=F32)
                        scores = jnp.concatenate([before, scores], axis=1)
                    top = jnp.max(scores, axis=1, keepdims=True)
                    prob = jnp.exp2((scores - top) * (head_dim ** -0.5 * LOG2E))
                    prob = (prob * (1.0 / jnp.sum(prob, axis=1, keepdims=True))).astype(BF16)
                    qkv[base:keys, lane(0)] = jnp.dot(prob, qkv[0:keys, lane(2 * width)], preferred_element_type=F32).astype(BF16)
                return carry
            lax.fori_loop(0, heads // 2, two, 0)

        def x_load(b):
            return pltpu.make_async_copy(recv.at[pl.ds(b * e_rows, e_rows), :], lhs.at[pl.ds(0, e_rows), :], lsem.at[0])

        def expert(b, mid):
            x_load(b).start()
            x_load(b).wait()
            last = b == E_BLOCKS - 1
            gate_up(lhs, he, experts_in, b * experts_in.tiles, ffn_in.go if last else experts_in.go, mid)
            tiles = d_model // TILE

            def put(i):
                k = lax.rem(i, 2)
                return pltpu.make_async_copy(ystage.at[k], y.at[pl.ds(b * e_rows, e_rows), at(i * TILE, TILE, TILE)], ysem.at[k])

            def keep(i, slot, acc):
                pl.when(i >= 2)(lambda: put(i - 2).wait())
                ystage[lax.rem(i, 2)] = acc.astype(BF16)
                put(i).start()
            follow = from_out if last else from_ed
            columns(he, e_rows, ed.shape[0], tiles, from_ed, keep, lambda i, slot: go(follow, i, slot))
            put(tiles - 2).wait()
            put(tiles - 1).wait()
            span = ep // E_BLOCKS
            for k in range(b * span, (b + 1) * span):
                (y_copy(k) if k else y_local).start()

        def project_out(p):
            for k in range(CHUNKS // PAIRS):
                arrived(c_second, p * (CHUNKS // PAIRS) + k)
            piece = pl.ds(p * pair_rows, pair_rows)
            here = pl.ds(0, pair_rows)
            loads = [pltpu.make_async_copy(src.at[piece, :], lhs.at[here, at(who * width, width, width)], lsem.at[k])
                     for k, (src, who) in enumerate(((c_r, right), (c_o, far), (c_l, left)))]
            loads.append(pltpu.make_async_copy(x.at[piece, at(me * width, width, width)], a_own.at[piece, :], lsem.at[4]))
            for cp in loads:
                cp.start()
            lhs[here, at(me * width, width, width)] = qkv[piece, 0:width]
            for cp in loads:
                cp.wait()

            def keep(i, slot, acc):
                block = (piece, at(i * TILE, TILE, TILE))
                a_own[block] = (a_own[block].astype(F32) + acc).astype(BF16)
            follow = from_ed if p < PAIRS - 1 else from_wd
            columns(lhs, pair_rows, d_model, width // TILE, from_out, keep, lambda i, slot: go(follow, i, slot))

        n_load(0).start()
        depth_block = 256
        pltpu.emit_pipeline(
            functools.partial(relay_kernel, heads),
            grid=(d_model // depth_block,),
            in_specs=[pl.BlockSpec((depth_block * heads, head_dim), lambda i: (i, 0))] * 3,
            out_specs=[pl.BlockSpec((depth_block, 3 * width), lambda i: (i, 0))],
        )(wq, wk, wv, wqkv)
        prime(from_qkv)
        project_in(0)
        for k in range(nt_ahead):
            experts_in.go(k, k)
        attend(0)
        start(c_first, 0)
        attend(1)
        start(c_first, 1)
        w_pair()
        project_in(1, w_done)
        c_forward(0)
        attend(2)
        c_forward(1)
        start(c_first, 2)
        attend(3)
        start(c_first, 3)
        project_out(0)
        start(a_first, 0)
        for k in range(1, ep):
            d_copy(k).wait_recv()
        d_local.wait()
        expert(0, lambda: c_forward(2))

        def late():
            a_forward(0)
            start(a_first, 1)
        c_forward(3)
        expert(1, late)
        project_out(1)
        for c in range(CHUNKS):
            sent(c_first, c)

    pl.run_scoped(
        first_half, pltpu.VMEM((max(pair_rows, e_rows), d_model), BF16), pltpu.VMEM((e_rows, ed.shape[0]), BF16),
        pltpu.VMEM((seq, 3 * width), BF16), pltpu.VMEM((2, e_rows, TILE), BF16))
    start(a_first, 2)

    def second_half(lhs, h, fbuf, a_in, sel, gates):
        held['fbuf'] = fbuf

        def reduce_on(c):
            for d, who in ((0, right), (1, left)):
                r_first(c, d).wait_recv()

                def add(k, carry, d=d, who=who):
                    block = (lax.rem(c, 2), at(who * quarter + d * q_half + k * 8, 8, 8), slice(None))
                    fbuf[block] = fbuf[block] + r1[lax.rem(c, 2), d, at(k * 8, 8, 8), :]
                    return carry
                lax.fori_loop(0, q_half // 8, add, 0)
            start(r_second, c)

        def o_local(c):
            return pltpu.make_async_copy(out_q.at[c], out.at[at(c * rows + me * quarter, quarter, quarter), :], osem.at[c])

        def finish(c):
            arrived(r_second, c)

            def add(k, carry):
                part = at(k * 16, 16, 16)
                total = fbuf[lax.rem(c, 2), at(me * quarter + k * 16, 16, 16), :] + (r2[lax.rem(c, 2), 0, part, :] + r2[lax.rem(c, 2), 1, part, :])
                out_q[c, part, :] = (a_mine[c, part, :].astype(F32) + total).astype(BF16)
                return carry
            lax.fori_loop(0, quarter // 16, add, 0)
            start(o_first, c)
            o_local(c).start()

        def o_forward(c):
            arrived(o_first, c)
            start(o_second, c)

        def from_back(i, slot):
            return pltpu.make_async_copy(back.at[:, at(i * TILE, TILE, TILE)], wb3.at[slot], sem3.at[slot])

        def copies_prime():
            for k in range(nn_ahead):
                from_back(k, k).start()

        def combine(c):
            tiles = d_model // TILE

            def step(i, carry):
                nxt = i + nn_ahead
                pl.when(nxt < tiles)(lambda: from_back(nxt, lax.rem(nxt, NN_SLOTS)).start())
                slot = lax.rem(i, NN_SLOTS)
                from_back(i, slot).wait()
                copies = jnp.dot(sel[...], wb3[slot], preferred_element_type=F32)
                block = (lax.rem(c, 2), slice(None), at(i * TILE, TILE, TILE))
                total = fbuf[block]
                for j in range(top_k):
                    total = total + gates[:, j:j + 1] * copies[j * rows:(j + 1) * rows]
                fbuf[block] = total
                return carry
            lax.fori_loop(0, tiles, step, 0)

        def ffn(c, carry):
            arrived(a_second, c)
            piece = at(c * rows, rows, rows)
            loads = [pltpu.make_async_copy(src.at[piece, :], a_in.at[k], lsem.at[k]) for k, src in enumerate((a_r, a_o, a_l))]
            for cp in loads:
                cp.start()
            for cp in loads:
                cp.wait()
            parts = ((None, me), (0, right), (1, far), (2, left))

            def norm(k, carry):
                block = at(k * 16, 16, 16)
                vals = [(a_own[at(c * rows + k * 16, 16, 16), :] if p is None else a_in[p, block, :]).astype(F32) for p, _ in parts]
                square = sum(jnp.sum(v * v, axis=1, keepdims=True) for v in vals)
                inv = lax.rsqrt(square / d_model + EPS)
                for v, (_, who) in zip(vals, parts):
                    cols = at(who * width, width, width)
                    lhs[block, cols] = (v * inv * gain[2:3, cols]).astype(BF16)
                return carry
            lax.fori_loop(0, rows // 16, norm, 0)
            for p, who in parts:
                mine = at(me * quarter, quarter, quarter)
                val = a_own[at(c * rows + me * quarter, quarter, quarter), :] if p is None else a_in[p, mine, :]
                a_mine[c, :, at(who * width, width, width)] = val
            table = jnp.transpose(route[:, piece])
            lane = lax.broadcasted_iota(jnp.int32, (rows, slots_all), 1).astype(F32)
            for j in range(top_k):
                sel[j * rows:(j + 1) * rows, :] = jnp.where(lane == table[:, j:j + 1], 1.0, 0.0).astype(BF16)
                gates[:, j:j + 1] = table[:, top_k + j:top_k + j + 1]

            def mid():
                @pl.when(c == 0)
                def _():
                    a_forward(1)
                    start(a_first, 3)
                pl.when(c >= 1)(lambda: reduce_on(c - 1))
            def after(i, slot):
                pl.when(c < CHUNKS - 1)(lambda: ffn_in.go(i, slot))
            gate_up(lhs, h, ffn_in, E_BLOCKS * experts_in.tiles + c * ffn_in.tiles, after, mid)
            pl.when(c == 0)(lambda: a_forward(2))

            @pl.when(c >= 2)
            def _():
                o_forward(c - 2)
                sent(r_first, c - 2)
                sent(r_second, c - 2)

            def keep(i, slot, acc):
                fbuf[lax.rem(c, 2), :, at(i * TILE, TILE, TILE)] = acc

            def then(i, slot):
                pl.when(c < CHUNKS - 1)(lambda: go(from_wd, i, slot))
            pl.when(c > 0)(copies_prime)
            columns(h, rows, wd.shape[0], d_model // TILE, from_wd, keep, then)

            @pl.when(c == 0)
            def _():
                a_forward(3)
                y_back()
                copies_prime()
            combine(c)
            start(r_first, c)
            pl.when(c >= 1)(lambda: finish(c - 1))
            return carry
        lax.fori_loop(0, CHUNKS, ffn, 0)
        reduce_on(CHUNKS - 1)
        o_forward(CHUNKS - 2)
        finish(CHUNKS - 1)
        o_forward(CHUNKS - 1)

        def drain(c, carry):
            arrived(o_second, c)
            o_local(c).wait()
            for make in (c_second, a_first, a_second, o_first, o_second):
                sent(make, c)

            @pl.when(c >= CHUNKS - 2)
            def _():
                sent(r_first, c)
                sent(r_second, c)
            return carry
        lax.fori_loop(0, CHUNKS, drain, 0)
        for k in range(1, ep):
            d_copy(k).wait_send()
            y_copy(k).wait_send()
        w_sent()

    pl.run_scoped(
        second_half, pltpu.VMEM((rows, d_model), BF16), pltpu.VMEM((rows, wd.shape[0]), BF16), pltpu.VMEM((2, rows, d_model), F32),
        pltpu.VMEM((3, rows, width), BF16), pltpu.VMEM((top_k * rows, slots_all), BF16), pltpu.VMEM((rows, top_k), F32))


def fused_layer(tp, ep, heads, top_k, n, wq, wk, wv, w_out, x, gains, wg, wu, wd, send, eg, eu, ed, route, cos, sin):
    seq, d_model = x.shape
    rows = seq // CHUNKS
    quarter = rows // tp
    width = d_model // tp
    hidden = wd.shape[0]
    slots_all = send.shape[0]
    any_spec = pl.BlockSpec(memory_space=pl.ANY)
    vmem_spec = pl.BlockSpec(memory_space=pltpu.VMEM)
    part = jax.ShapeDtypeStruct((seq, width), BF16)
    copies = jax.ShapeDtypeStruct((slots_all, d_model), BF16)
    outs = pl.pallas_call(
        functools.partial(layer_kernel, tp, ep, heads, top_k),
        out_shape=[jax.ShapeDtypeStruct((seq, d_model), BF16), jax.ShapeDtypeStruct((d_model, 3 * width), BF16)] + [part] * 6
        + [jax.ShapeDtypeStruct((tp, w_out.shape[0], width), BF16)] + [copies] * 3,
        in_specs=[any_spec] * 6 + [vmem_spec] + [any_spec] * 7 + [vmem_spec] * 3,
        out_specs=[any_spec] * 12,
        scratch_shapes=[
            pltpu.VMEM((2, 2, quarter // 2, d_model), F32),
            pltpu.VMEM((2, 2, quarter, d_model), F32),
            pltpu.VMEM((seq, width), BF16),
            pltpu.VMEM((CHUNKS, quarter, d_model), BF16),
            pltpu.VMEM((CHUNKS, quarter, d_model), BF16),
            pltpu.VMEM((NT_SLOTS, 2, TILE, d_model), BF16),
            pltpu.VMEM((NN_SLOTS, d_model, TILE), BF16),
            pltpu.VMEM((NN_SLOTS, slots_all, TILE), BF16),
            pltpu.SemaphoreType.DMA((8, CHUNKS, 2)),
            pltpu.SemaphoreType.DMA((8, CHUNKS, 2)),
            pltpu.SemaphoreType.DMA((ep,)),
            pltpu.SemaphoreType.DMA((ep,)),
            pltpu.SemaphoreType.DMA((ep,)),
            pltpu.SemaphoreType.DMA((ep,)),
            pltpu.SemaphoreType.DMA((2,)),
            pltpu.SemaphoreType.DMA((2, tp)),
            pltpu.SemaphoreType.DMA((2, tp)),
            pltpu.SemaphoreType.DMA((NT_SLOTS, 2)),
            pltpu.SemaphoreType.DMA((NN_SLOTS, 4)),
            pltpu.SemaphoreType.DMA((NN_SLOTS,)),
            pltpu.SemaphoreType.DMA((5,)),
            pltpu.SemaphoreType.DMA((CHUNKS,)),
        ],
        compiler_params=pltpu.CompilerParams(collective_id=0, has_side_effects=True, vmem_limit_bytes=67043328),
        cost_estimate=pl.CostEstimate(flops=6 * seq * d_model * hidden, bytes_accessed=300 * 2 ** 20, transcendentals=seq * hidden),
    )(n, wq, wk, wv, w_out, x, gains, wg, wu, wd, send, eg, eu, ed, route, cos, sin)
    return outs[0]


def solution(mesh):
    tok_spec = P(('dp', 'ep'), None, None)
    col_spec = P(None, 'tp', None)
    exp_spec = P('ep', None, None)
    in_specs = (tok_spec, tok_spec, tok_spec, P(None), col_spec, col_spec, col_spec, P('tp', None, None), P(None), P(None, 'tp'), P(None, 'tp'), P('tp', None), P(None), P(None, None), exp_spec, exp_spec, exp_spec)
    tp = mesh.shape['tp']
    ep = mesh.shape['ep']

    def layer_local(hidden_in, expert_ids, slot_ids, attn_gain, w_query, w_key, w_value, w_out, ffn_gain, w_gate, w_up, w_down, moe_gain, w_router, exp_gate, exp_up, exp_down):
        _, seq, d_model = hidden_in.shape
        heads, head_dim = w_query.shape[1:]
        experts = w_router.shape[1]
        top_k = expert_ids.shape[2]
        cap = 3 * seq * top_k // (2 * experts)
        sub = cap // tp
        x = hidden_in[0]
        gains = jnp.stack([attn_gain, moe_gain, ffn_gain]).astype(F32)
        n, route, send = prepare(tp, x, gains, w_router.T, expert_ids[0].T, slot_ids[0].T, experts * sub)
        cos, sin = rope_tables(seq, head_dim)
        flat = lambda w: w.reshape(d_model * heads, head_dim)
        out = fused_layer(tp, ep, heads, top_k, n, flat(w_query), flat(w_key), flat(w_value), w_out.reshape(heads * head_dim, d_model), x,
                          gains, w_gate.T, w_up.T, w_down, send,
                          exp_gate[0].T, exp_up[0].T, exp_down[0], route, cos, sin)
        return out[None]

    return jax.shard_map(layer_local, mesh=mesh, in_specs=in_specs, out_specs=tok_spec, check_vma=False)
```

time: 1710 us -> 446 us (0.26)
  waiting for transfers between devices: 714 us -> 0 us
  Pallas kernels: 0 us -> 434 us
  local copies, waits for them, and re-layouts: 347 us -> 10 us
  matrix products: 322 us -> 0 us
  other arithmetic: 286 us -> 0.7 us
    pallas_call x0 -> x2, Pallas kernels: none -> 434 us  [the longest x1 415 us: fused_layer(): pl.pallas_call(functools.partial(layer_kernel, tp, ep, heads, top_k), out...]
    all_to_all x2 -> x0, waiting for transfers between devices: 430 us -> none  [the longest x1 272 us: moe_branch(): recv_buf = lax.all_to_all(send_buf, 'ep', 0, 1, tiled=True)]
    psum x2 -> x0, waiting for transfers between devices: 284 us -> none  [the longest x1 284 us: dense_branch(): attn_sum = lax.psum(attn_part, 'tp')]
    dot_general x10 -> x0, matrix products: 281 us -> none  [the longest x1 44.9 us: expert_swiglu(): jnp.einsum('erf,efd->erd', hidden_act, exp_down, preferred_element_type=j...]
    unnamed x3 -> x0, other arithmetic: 152 us -> none
    unnamed x50 -> x1, local copies, waits for them, and re-layouts: 152 us -> 7.89 us
    gather x7 -> x0, local copies, waits for them, and re-layouts: 127 us -> none  [the longest x2 67.3 us: moe_branch(): per_copy = jnp.take(returned, flat_pos, axis=0)]
    reduce_sum x4 -> x0, other arithmetic: 85.6 us -> none  [the longest x1 64.2 us: moe_branch(): moe_out = jnp.sum(gates[:, :, None] * per_copy.astype(jnp.float32), axis=1)]
  transfers between devices with their start and end apart: 4 -> 0, of which waited for: 3 -> 0; matrix products, arithmetic and copies ran while one was open for 21% -> 0% of each run, Pallas kernels for 0% -> 0%
where the time goes in v2:
time: 446 us; the launch traced here: 445 us
  Pallas kernels  434 us (97%)
  local copies, waits for them, and re-layouts  10 us (2%)
    pallas_call x1, Pallas kernels, fused_layer(): pl.pallas_call(functools.partial(layer_kernel, tp, ep, heads, top_k), out...  415 us
    pallas_call x1, Pallas kernels, prepare(): pl.pallas_call(functools.partial(prep_kernel, tp, blocks), grid=(blocks +...  18.6 us

profile of v2, /device:TPU:97, one launch (start us, length us, event | category | flops | bytes accessed | tf_op | source)
XLA Modules:
  0.0 444.7 jit_solution(813299176957686414)
XLA Ops:
  0.0 0.7 stack.12
  0.7 0.7 stack.14
  1.4 0.7 stack.13
  2.1 0.7 maximum_convert_fusion.gain_ref.gain
  2.8 18.6 %shard_map.181 = (bf16[1024,4096]{1,0:T(8,128)(2,1)}, f32[8,1024]{1,0:T(8,128)}, bf16[768,4096]{1,0:T(8,128)(2,1)}) custom-call(bf16[1024,4096]{1,0:T(8,128)(2,1)} %bitcast.28, f32[3,4096]{1,0:T(4,128)} %maximum_convert_fusion.gain_ref.gain, bf16[8,4096]{1,0:T(8,128)(2,1)} %bitcast.34, s32[2,1024]{1,0:T(2,128)} %bitcast.35, s32[2,1024]{1,0:T(2,128)} %bitcast.36), custom_call_target="tpu_custom_call" | custom-call | flops 6442450944 | bytes 25165824 | tf_op jit(solution)/shard_map/pallas_call | solution.py:74
  21.4 415.4 %shard_map.182 = (bf16[1024,4096]{1,0:T(8,128)(2,1)}, bf16[4096,3072]{1,0:T(8,128)(2,1)}, bf16[1024,1024]{1,0:T(8,128)(2,1)}, bf16[1024,1024]{1,0:T(8,128)(2,1)}...) custom-call(bf16[1024,4096]{1,0:T(8,128)(2,1)} %get-tuple-element.9., ...), custom_call_target="tpu_custom_call" | custom-call | flops 69256347648 | bytes 314572800 | tf_op jit(solution)/shard_map/pallas_call | solution.py:656
  436.8 7.9 %copy.21 = bf16[1,1024,4096]{2,1,0:T(8,128)(2,1)} copy(bf16[1,1024,4096]{2,1,0:T(8,128)(2,1)} %bitcast.22) | data formatting | bytes 16777216

commit v3 on v2

--- a/solution.py
+++ b/solution.py
@@ -22,70 +22,8 @@
     return np.concatenate([cos, cos], axis=1), np.concatenate([-sin, sin], axis=1)
 
 
-def prep_kernel(tp, blocks, x_ref, gain_ref, wr_ref, ids_ref, slots_ref, n_ref, route_ref, send_ref, u_ref, pick_ref):
-    step = pl.program_id(0)
-    size, cols = x_ref.shape[0], send_ref.shape[1]
-    top_k = ids_ref.shape[0]
-    slots_all = send_ref.shape[0]
-    sub = slots_all // wr_ref.shape[0]
-
-    @pl.when(step < blocks)
-    def _():
-        x = x_ref[...].astype(F32)
-        unit = x * lax.rsqrt(jnp.mean(x * x, axis=-1, keepdims=True) + EPS)
-        n_ref[...] = (unit * gain_ref[0:1, :]).astype(BF16)
-        u = (unit * gain_ref[1:2, :]).astype(BF16)
-        mine = pl.ds(pl.multiple_of(step * size, size), size)
-        u_ref[mine, :] = u
-        logits = lax.dot_general(wr_ref[...], u, (((1,), (1,)), ((), ())), preferred_element_type=F32)
-        expert = lax.broadcasted_iota(jnp.int32, logits.shape, 0)
-        picked = [jnp.sum(jnp.where(expert == ids_ref[j:j + 1, mine], logits, 0.0), axis=0, keepdims=True) for j in range(top_k)]
-        top = functools.reduce(jnp.maximum, picked)
-        weights = [jnp.exp(p - top) for p in picked]
-        total = sum(weights)
-        for j in range(top_k):
-            route_ref[top_k + j:top_k + j + 1, mine] = weights[j] / total
-
-    @pl.when(step == blocks)
-    def _():
-        rank = lax.axis_index('tp')
-        rows = lax.broadcasted_iota(jnp.int32, pick_ref.shape, 0)
-        hit = None
-        for j in range(top_k):
-            slot = slots_ref[j:j + 1, :]
-            row_of = jnp.where(lax.rem(slot, tp) == rank, ids_ref[j:j + 1, :] * sub + lax.div(slot, tp), -1)
-            route_ref[j:j + 1, :] = row_of.astype(F32)
-            match = rows == row_of
-            hit = match if hit is None else hit | match
-        pick_ref[...] = jnp.where(hit, 1.0, 0.0).astype(BF16)
-
-    @pl.when(step >= blocks)
-    def _():
-        part = pl.ds(pl.multiple_of((step - blocks) * cols, cols), cols)
-        send_ref[...] = jnp.dot(pick_ref[...], u_ref[:, part], preferred_element_type=F32).astype(BF16)
-
-
-def prepare(tp, x, gains, router, ids, slots, slots_all):
-    seq, d_model = x.shape
-    size, cols = 256, 512
-    blocks, parts = seq // size, d_model // cols
-    token = lambda i: (jnp.minimum(i, blocks - 1), 0)
-    fixed = lambda i: (0, 0)
-    return pl.pallas_call(
-        functools.partial(prep_kernel, tp, blocks),
-        grid=(blocks + parts,),
-        in_specs=[pl.BlockSpec((size, d_model), token), pl.BlockSpec(gains.shape, fixed), pl.BlockSpec(router.shape, fixed),
-                  pl.BlockSpec(ids.shape, fixed), pl.BlockSpec(slots.shape, fixed)],
-        out_specs=[pl.BlockSpec((size, d_model), token), pl.BlockSpec((8, seq), fixed),
-                   pl.BlockSpec((slots_all, cols), lambda i: (0, jnp.maximum(i - blocks, 0)))],
-        out_shape=[jax.ShapeDtypeStruct((seq, d_model), BF16), jax.ShapeDtypeStruct((8, seq), F32), jax.ShapeDtypeStruct((slots_all, d_model), BF16)],
-        scratch_shapes=[pltpu.VMEM((seq, d_model), BF16), pltpu.VMEM((slots_all, seq), BF16)],
-        cost_estimate=pl.CostEstimate(flops=2 * slots_all * seq * d_model, bytes_accessed=6 * seq * d_model, transcendentals=0),
-    )(x, gains, router, ids, slots)
-
-
-def relay_kernel(heads, *refs):
-    sources, o_ref = refs[:-1], refs[-1]
+def relay_kernel(heads, acc, *refs):
+    n_ref, sources, o_ref = refs[0], refs[1:-1], refs[-1]
     depth, head_dim = o_ref.shape[0], sources[0].shape[1]
     block = 256
     span = block // heads
@@ -98,6 +36,10 @@
             for k in range(heads):
                 lane = (w * heads + k) * head_dim
                 o_ref[g * span:(g + 1) * span, lane:lane + head_dim] = moved[k * span:(k + 1) * span]
+    wide = 512
+    for t in range(o_ref.shape[1] // wide):
+        cols = pl.ds(t * wide, wide)
+        acc[:, cols] += jnp.dot(n_ref[...], o_ref[:, cols], preferred_element_type=F32)
 
 
 TILE = 256
@@ -108,15 +50,16 @@
 NN_SLOTS = 4
 
 
-def layer_kernel(tp, ep, heads, top_k, n, wq, wk, wv, w_out, x, gain, wg, wu, wd, send, eg, eu, ed, route, cos_ref, sin_ref,
-                 out, wqkv, c_l, c_r, c_o, a_l, a_r, a_o, wx, recv, y, back,
-                 r1, r2, a_own, a_mine, out_q, wb1, wb2, wb3,
+def layer_kernel(tp, ep, heads, wq, wk, wv, w_out, x, gain, wg, wu, wd, eg, eu, ed, wr, ids, slots, cos_ref, sin_ref,
+                 out, n, send, wqkv, c_l, c_r, c_o, a_l, a_r, a_o, wx, recv, y, back,
+                 route, r1, r2, a_own, a_mine, out_q, wb1, wb2, wb3,
                  send_sem, recv_sem, dsend, drecv, ysend, yrecv, ysem, wsend, wrecv, sem1, sem2, sem3, lsem, osem):
     seq, d_model = out.shape
     rows = seq // CHUNKS
     quarter = rows // tp
     width = d_model // tp
     slots_all = recv.shape[0]
+    top_k = ids.shape[0]
     sub = slots_all // ep
     me = lax.axis_index('tp')
     my_e = lax.axis_index('ep')
@@ -165,8 +108,15 @@
     def r_second(c, d):
         return remote(5, c, d, held['fbuf'].at[lax.rem(c, 2), at((right, left)[d] * quarter, quarter, quarter), :], r2.at[lax.rem(c, 2), d])
 
+    def o_half(kind, c, d, part):
+        rows_of = c * rows + me * quarter + part * q_half
+        return remote(kind, c, d, out_q.at[c, pl.ds(part * q_half, q_half), :], out.at[at(rows_of, q_half, q_half), :])
+
     def o_first(c, d):
-        return remote(6, c, d, out_q.at[c], out.at[at(c * rows + me * quarter, quarter, quarter), :])
+        return o_half(6, c, d, d)
+
+    def o_other(c, d):
+        return o_half(8, c, d, 1 - d)
 
     def o_second(c, d):
         piece = at(c * rows + (left, right)[d] * quarter + d * q_half, q_half, q_half)
@@ -277,7 +227,7 @@
         for j in range(nn_ahead):
             go(fetch, j, j)
 
-    def columns(left_ref, m, depth, tiles, fetch, use, then=None):
+    def columns(left_ref, m, depth, tiles, fetch, use, then=None, off=0):
         def step(i, carry):
             nxt = i + nn_ahead
             ahead = lax.rem(nxt, NN_SLOTS)
@@ -287,7 +237,7 @@
             slot = lax.rem(i, NN_SLOTS)
             for cp in fetch(i, slot):
                 cp.wait()
-            use(i, slot, jnp.dot(left_ref[:m, :depth], wb2[slot, :depth, :], preferred_element_type=F32))
+            use(i, slot, jnp.dot(left_ref[off:off + m, :depth], wb2[slot, :depth, :], preferred_element_type=F32))
             return carry
 
         lax.fori_loop(0, tiles, step, 0)
@@ -315,68 +265,143 @@
         arrived(c_first, c)
         start(c_second, c)
 
-    def d_copy(k):
-        peer = lax.rem(my_e + k, ep)
+    chips = ep // 2
+    my_chip = my_e // 2
+    order = sorted(((m, flip) for m in range(chips) for flip in range(2)), key=lambda v: (-min(v[0], chips - v[0]), -v[1]))
+    place = {v: q for q, v in enumerate(order)}
+    others = range(ep - 1)
+
+    def peer_of(q):
+        m, flip = order[q]
+        return 2 * lax.rem(my_chip + m, chips) + (1 - core if flip else core)
+
+    def back_place(q):
+        m, flip = order[q]
+        return place[((chips - m) % chips, flip)]
+
+    def d_copy(q):
+        peer = peer_of(q)
         return pltpu.make_async_remote_copy(
-            src_ref=send.at[at(peer * sub, sub, sub), :], dst_ref=recv.at[pl.ds((ep - k) * sub, sub), :],
-            send_sem=dsend.at[k], recv_sem=drecv.at[k], device_id={'ep': peer}, device_id_type=MESH)
+            src_ref=send.at[at(peer * sub, sub, sub), :], dst_ref=recv.at[pl.ds(back_place(q) * sub, sub), :],
+            send_sem=dsend.at[q], recv_sem=drecv.at[q], device_id={'ep': peer}, device_id_type=MESH)
 
     own_rows = at(my_e * sub, sub, sub)
-    d_local = pltpu.make_async_copy(send.at[own_rows, :], recv.at[pl.ds(0, sub), :], dsend.at[0])
-
-    def y_copy(k):
+
+    def y_copy(q):
         return pltpu.make_async_remote_copy(
-            src_ref=y.at[pl.ds(k * sub, sub), :], dst_ref=back.at[own_rows, :],
-            send_sem=ysend.at[k], recv_sem=yrecv.at[k], device_id={'ep': lax.rem(my_e + k, ep)}, device_id_type=MESH)
-
-    y_local = pltpu.make_async_copy(y.at[pl.ds(0, sub), :], back.at[own_rows, :], ysend.at[0])
+            src_ref=y.at[pl.ds(q * sub, sub), :], dst_ref=back.at[own_rows, :],
+            send_sem=ysend.at[q], recv_sem=yrecv.at[q], device_id={'ep': peer_of(q)}, device_id_type=MESH)
+
 
     def y_back():
-        for k in range(1, ep):
-            y_copy(k).wait_recv()
-        y_local.wait()
+        for q in others:
+            y_copy(q).wait_recv()
 
     def a_forward(c):
         arrived(a_first, c)
         start(a_second, c)
 
     w_start()
-    for k in range(1, ep):
-        d_copy(k).start()
-    d_local.start()
+
+    def prepare(u, pick, x_in, n_out, piled):
+        size = x_in.shape[1]
+        blocks = seq // size
+
+        def x_get(i, k):
+            return pltpu.make_async_copy(x.at[at(i * size, size, size), :], x_in.at[k], sem2.at[k, 0])
+
+        def n_put(i, k):
+            return pltpu.make_async_copy(n_out.at[k], n.at[at(i * size, size, size), :], sem3.at[k])
+
+        x_get(0, 0).start()
+
+        def norm(i, carry):
+            k = lax.rem(i, 2)
+            pl.when(i + 1 < blocks)(lambda: x_get(i + 1, 1 - k).start())
+            pl.when(i >= 2)(lambda: n_put(i - 2, k).wait())
+            x_get(i, k).wait()
+            mine = at(i * size, size, size)
+            val = x_in[k].astype(F32)
+            unit = val * lax.rsqrt(jnp.mean(val * val, axis=-1, keepdims=True) + EPS)
+            n_out[k] = (unit * gain[0:1, :]).astype(BF16)
+            n_put(i, k).start()
+            row = (unit * gain[1:2, :]).astype(BF16)
+            u[mine, :] = row
+            logits = lax.dot_general(wr[...], row, (((1,), (1,)), ((), ())), preferred_element_type=F32)
+            expert = lax.broadcasted_iota(jnp.int32, logits.shape, 0)
+            picked = [jnp.sum(jnp.where(expert == ids[j:j + 1, mine], logits, 0.0), axis=0, keepdims=True) for j in range(top_k)]
+            top = functools.reduce(jnp.maximum, picked)
+            weights = [jnp.exp(p - top) for p in picked]
+            total = sum(weights)
+            for j in range(top_k):
+                route[top_k + j:top_k + j + 1, mine] = weights[j] / total
+            return carry
+        lax.fori_loop(0, blocks, norm, 0)
+        rows_all = lax.broadcasted_iota(jnp.int32, pick.shape, 0)
+        hit = None
+        for j in range(top_k):
+            slot = slots[j:j + 1, :]
+            row_of = jnp.where(lax.rem(slot, tp) == me, ids[j:j + 1, :] * sub + lax.div(slot, tp), -1)
+            route[j:j + 1, :] = row_of.astype(F32)
+            match = rows_all == row_of
+            hit = match if hit is None else hit | match
+        pick[...] = jnp.where(hit, 1.0, 0.0).astype(BF16)
+        cols = piled.shape[2]
+        parts = d_model // cols
+
+        def put(i, k):
+            return pltpu.make_async_copy(piled.at[k], send.at[:, at(i * cols, cols, cols)], sem1.at[k, 0])
+
+        def gather(i, carry):
+            k = lax.rem(i, 2)
+            pl.when(i >= 2)(lambda: put(i - 2, k).wait())
+            piled[k] = jnp.dot(pick[...], u[:, at(i * cols, cols, cols)], preferred_element_type=F32).astype(BF16)
+            put(i, k).start()
+            return carry
+        lax.fori_loop(0, parts, gather, 0)
+        for i in range(parts - 2, parts):
+            put(i, i % 2).wait()
+        for i in range(blocks - 2, blocks):
+            n_put(i, i % 2).wait()
+
+    tokens = 128
+    pl.run_scoped(
+        prepare, pltpu.VMEM((seq, d_model), BF16), pltpu.VMEM((slots_all, seq), BF16), pltpu.VMEM((2, tokens, d_model), BF16),
+        pltpu.VMEM((2, tokens, d_model), BF16), pltpu.VMEM((2, slots_all, 512), BF16))
+    for q in others:
+        d_copy(q).start()
 
     head_dim = width // heads
     low = head_dim // 2
 
-    def first_half(lhs, he, qkv, ystage):
+    def first_half(lhs, he, qkv, ystage, acc):
         held['qkv'] = qkv
 
         def n_load(p):
             return pltpu.make_async_copy(n.at[pl.ds(p * pair_rows, pair_rows), :], lhs.at[pl.ds(0, pair_rows), :], lsem.at[0])
 
-        def project_in(p, between=None):
-            piece = pl.ds(p * pair_rows, pair_rows)
-            n_load(p).wait()
-
-            def rotate(val):
-                parts = []
-                for k in range(TILE // head_dim):
-                    one = val[:, k * head_dim:(k + 1) * head_dim]
-                    parts.append(one * cos_ref[piece, :] + pltpu.roll(one, low, 1) * sin_ref[piece, :])
-                return jnp.concatenate(parts, axis=1)
-
-            def keep(i, slot, acc):
-                acc = jnp.where(i < 2 * width // TILE, rotate(acc), acc)
-                qkv[piece, at(i * TILE, TILE, TILE)] = acc.astype(BF16)
-            follow = from_qkv if p < PAIRS - 1 else from_out
+        def rotate(val, piece):
+            parts = []
+            for k in range(TILE // head_dim):
+                one = val[:, k * head_dim:(k + 1) * head_dim]
+                parts.append(one * cos_ref[piece, :] + pltpu.roll(one, low, 1) * sin_ref[piece, :])
+            return jnp.concatenate(parts, axis=1)
+
+        def settle(piece, i, val):
+            val = jnp.where(i < 2 * width // TILE, rotate(val, piece), val)
+            qkv[piece, at(i * TILE, TILE, TILE)] = val.astype(BF16)
+
+        def project_in(start_row, count, off, follow, between=None):
+            piece = pl.ds(start_row, count)
+
+            def keep(i, slot, val):
+                settle(piece, i, val)
 
             def then(i, slot):
                 if between is not None:
                     pl.when(i == 0)(between)
                 go(follow, i, slot)
-            columns(lhs, pair_rows, d_model, 3 * width // TILE, from_qkv, keep, then)
-            if p < PAIRS - 1:
-                n_load(p + 1).start()
+            columns(lhs, count, d_model, 3 * width // TILE, from_qkv, keep, then, off)
 
         def attend(c):
             base = c * rows
@@ -403,30 +428,52 @@
             lax.fori_loop(0, heads // 2, two, 0)
 
         def x_load(b):
-            return pltpu.make_async_copy(recv.at[pl.ds(b * e_rows, e_rows), :], lhs.at[pl.ds(0, e_rows), :], lsem.at[0])
+            far = e_rows - (sub if b == E_BLOCKS - 1 else 0)
+            copies = [pltpu.make_async_copy(recv.at[pl.ds(b * e_rows, far), :], lhs.at[pl.ds(0, far), :], lsem.at[0])]
+            if far < e_rows:
+                copies.append(pltpu.make_async_copy(send.at[own_rows, :], lhs.at[pl.ds(far, sub), :], lsem.at[1]))
+            return copies
 
         def expert(b, mid):
-            x_load(b).start()
-            x_load(b).wait()
+            loads = x_load(b)
+            for cp in loads:
+                cp.start()
+            for cp in loads:
+                cp.wait()
             last = b == E_BLOCKS - 1
             gate_up(lhs, he, experts_in, b * experts_in.tiles, ffn_in.go if last else experts_in.go, mid)
             tiles = d_model // TILE
 
+            far = e_rows - (sub if last else 0)
+
+            def puts(i):
+                k = lax.rem(i, 2)
+                cols = at(i * TILE, TILE, TILE)
+                copies = [pltpu.make_async_copy(ystage.at[k, pl.ds(0, far), :], y.at[pl.ds(b * e_rows, far), cols], ysem.at[k, 0])]
+                if last:
+                    copies.append(pltpu.make_async_copy(ystage.at[k, pl.ds(far, sub), :], back.at[own_rows, cols], ysem.at[k, 1]))
+                return copies
+
             def put(i):
-                k = lax.rem(i, 2)
-                return pltpu.make_async_copy(ystage.at[k], y.at[pl.ds(b * e_rows, e_rows), at(i * TILE, TILE, TILE)], ysem.at[k])
+                for cp in puts(i):
+                    cp.start()
+
+            def put_wait(i):
+                for cp in puts(i):
+                    cp.wait()
 
             def keep(i, slot, acc):
-                pl.when(i >= 2)(lambda: put(i - 2).wait())
+                pl.when(i >= 2)(lambda: put_wait(i - 2))
                 ystage[lax.rem(i, 2)] = acc.astype(BF16)
-                put(i).start()
+                put(i)
             follow = from_out if last else from_ed
             columns(he, e_rows, ed.shape[0], tiles, from_ed, keep, lambda i, slot: go(follow, i, slot))
-            put(tiles - 2).wait()
-            put(tiles - 1).wait()
+            put_wait(tiles - 2)
+            put_wait(tiles - 1)
             span = ep // E_BLOCKS
             for k in range(b * span, (b + 1) * span):
-                (y_copy(k) if k else y_local).start()
+                if k < ep - 1:
+                    y_copy(k).start()
 
         def project_out(p):
             for k in range(CHUNKS // PAIRS):
@@ -448,41 +495,51 @@
             follow = from_ed if p < PAIRS - 1 else from_wd
             columns(lhs, pair_rows, d_model, width // TILE, from_out, keep, lambda i, slot: go(follow, i, slot))
 
-        n_load(0).start()
+        second_load = pltpu.make_async_copy(n.at[pl.ds(rows, rows), :], lhs.at[pl.ds(rows, rows), :], lsem.at[0])
+        second_load.start()
+        acc[...] = jnp.zeros_like(acc)
         depth_block = 256
         pltpu.emit_pipeline(
-            functools.partial(relay_kernel, heads),
+            functools.partial(relay_kernel, heads, acc),
             grid=(d_model // depth_block,),
-            in_specs=[pl.BlockSpec((depth_block * heads, head_dim), lambda i: (i, 0))] * 3,
+            in_specs=[pl.BlockSpec((rows, depth_block), lambda i: (0, i), pipeline_mode=pl.Buffered(3))]
+            + [pl.BlockSpec((depth_block * heads, head_dim), lambda i: (i, 0), pipeline_mode=pl.Buffered(3))] * 3,
             out_specs=[pl.BlockSpec((depth_block, 3 * width), lambda i: (i, 0))],
-        )(wq, wk, wv, wqkv)
+        )(n, wq, wk, wv, wqkv)
         prime(from_qkv)
-        project_in(0)
+
+        def settle_first(i, carry):
+            settle(pl.ds(0, rows), i, acc[:, at(i * TILE, TILE, TILE)])
+            return carry
+        lax.fori_loop(0, 3 * width // TILE, settle_first, 0)
+        attend(0)
+        start(c_first, 0)
+        second_load.wait()
+        project_in(rows, rows, rows, from_qkv)
+        n_load(1).start()
+        attend(1)
+        start(c_first, 1)
         for k in range(nt_ahead):
             experts_in.go(k, k)
-        attend(0)
-        start(c_first, 0)
-        attend(1)
-        start(c_first, 1)
         w_pair()
-        project_in(1, w_done)
+        n_load(1).wait()
         c_forward(0)
+        project_in(2 * rows, 2 * rows, 0, from_out, w_done)
+        c_forward(1)
         attend(2)
-        c_forward(1)
         start(c_first, 2)
         attend(3)
         start(c_first, 3)
         project_out(0)
         start(a_first, 0)
-        for k in range(1, ep):
-            d_copy(k).wait_recv()
-        d_local.wait()
+        for q in others:
+            d_copy(q).wait_recv()
         expert(0, lambda: c_forward(2))
+        c_forward(3)
 
         def late():
             a_forward(0)
             start(a_first, 1)
-        c_forward(3)
         expert(1, late)
         project_out(1)
         for c in range(CHUNKS):
@@ -490,7 +547,8 @@
 
     pl.run_scoped(
         first_half, pltpu.VMEM((max(pair_rows, e_rows), d_model), BF16), pltpu.VMEM((e_rows, ed.shape[0]), BF16),
-        pltpu.VMEM((seq, 3 * width), BF16), pltpu.VMEM((2, e_rows, TILE), BF16))
+        pltpu.VMEM((seq, 3 * width), BF16), pltpu.VMEM((2, e_rows, TILE), BF16),
+        pltpu.VMEM((rows, 3 * width), F32))
     start(a_first, 2)
 
     def second_half(lhs, h, fbuf, a_in, sel, gates):
@@ -520,6 +578,7 @@
                 return carry
             lax.fori_loop(0, quarter // 16, add, 0)
             start(o_first, c)
+            start(o_other, c)
             o_local(c).start()
 
         def o_forward(c):
@@ -622,8 +681,9 @@
 
         def drain(c, carry):
             arrived(o_second, c)
+            arrived(o_other, c)
             o_local(c).wait()
-            for make in (c_second, a_first, a_second, o_first, o_second):
+            for make in (c_second, a_first, a_second, o_first, o_other, o_second):
                 sent(make, c)
 
             @pl.when(c >= CHUNKS - 2)
@@ -632,9 +692,9 @@
                 sent(r_second, c)
             return carry
         lax.fori_loop(0, CHUNKS, drain, 0)
-        for k in range(1, ep):
-            d_copy(k).wait_send()
-            y_copy(k).wait_send()
+        for q in others:
+            d_copy(q).wait_send()
+            y_copy(q).wait_send()
         w_sent()
 
     pl.run_scoped(
@@ -642,24 +702,24 @@
         pltpu.VMEM((3, rows, width), BF16), pltpu.VMEM((top_k * rows, slots_all), BF16), pltpu.VMEM((rows, top_k), F32))
 
 
-def fused_layer(tp, ep, heads, top_k, n, wq, wk, wv, w_out, x, gains, wg, wu, wd, send, eg, eu, ed, route, cos, sin):
+def fused_layer(tp, ep, heads, slots_all, wq, wk, wv, w_out, x, gains, wg, wu, wd, eg, eu, ed, router, ids, slots, cos, sin):
     seq, d_model = x.shape
     rows = seq // CHUNKS
     quarter = rows // tp
     width = d_model // tp
     hidden = wd.shape[0]
-    slots_all = send.shape[0]
     any_spec = pl.BlockSpec(memory_space=pl.ANY)
     vmem_spec = pl.BlockSpec(memory_space=pltpu.VMEM)
     part = jax.ShapeDtypeStruct((seq, width), BF16)
     copies = jax.ShapeDtypeStruct((slots_all, d_model), BF16)
     outs = pl.pallas_call(
-        functools.partial(layer_kernel, tp, ep, heads, top_k),
-        out_shape=[jax.ShapeDtypeStruct((seq, d_model), BF16), jax.ShapeDtypeStruct((d_model, 3 * width), BF16)] + [part] * 6
+        functools.partial(layer_kernel, tp, ep, heads),
+        out_shape=[jax.ShapeDtypeStruct((seq, d_model), BF16)] * 2 + [copies, jax.ShapeDtypeStruct((d_model, 3 * width), BF16)] + [part] * 6
         + [jax.ShapeDtypeStruct((tp, w_out.shape[0], width), BF16)] + [copies] * 3,
-        in_specs=[any_spec] * 6 + [vmem_spec] + [any_spec] * 7 + [vmem_spec] * 3,
-        out_specs=[any_spec] * 12,
+        in_specs=[any_spec] * 5 + [vmem_spec] + [any_spec] * 6 + [vmem_spec] * 5,
+        out_specs=[any_spec] * 14,
         scratch_shapes=[
+            pltpu.VMEM((8, seq), F32),
             pltpu.VMEM((2, 2, quarter // 2, d_model), F32),
             pltpu.VMEM((2, 2, quarter, d_model), F32),
             pltpu.VMEM((seq, width), BF16),
@@ -668,13 +728,13 @@
             pltpu.VMEM((NT_SLOTS, 2, TILE, d_model), BF16),
             pltpu.VMEM((NN_SLOTS, d_model, TILE), BF16),
             pltpu.VMEM((NN_SLOTS, slots_all, TILE), BF16),
-            pltpu.SemaphoreType.DMA((8, CHUNKS, 2)),
-            pltpu.SemaphoreType.DMA((8, CHUNKS, 2)),
+            pltpu.SemaphoreType.DMA((9, CHUNKS, 2)),
+            pltpu.SemaphoreType.DMA((9, CHUNKS, 2)),
             pltpu.SemaphoreType.DMA((ep,)),
             pltpu.SemaphoreType.DMA((ep,)),
             pltpu.SemaphoreType.DMA((ep,)),
             pltpu.SemaphoreType.DMA((ep,)),
-            pltpu.SemaphoreType.DMA((2,)),
+            pltpu.SemaphoreType.DMA((2, 2)),
             pltpu.SemaphoreType.DMA((2, tp)),
             pltpu.SemaphoreType.DMA((2, tp)),
             pltpu.SemaphoreType.DMA((NT_SLOTS, 2)),
@@ -685,7 +745,7 @@
         ],
         compiler_params=pltpu.CompilerParams(collective_id=0, has_side_effects=True, vmem_limit_bytes=67043328),
         cost_estimate=pl.CostEstimate(flops=6 * seq * d_model * hidden, bytes_accessed=300 * 2 ** 20, transcendentals=seq * hidden),
-    )(n, wq, wk, wv, w_out, x, gains, wg, wu, wd, send, eg, eu, ed, route, cos, sin)
+    )(wq, wk, wv, w_out, x, gains, wg, wu, wd, eg, eu, ed, router, ids, slots, cos, sin)
     return outs[0]
 
 
@@ -706,12 +766,11 @@
         sub = cap // tp
         x = hidden_in[0]
         gains = jnp.stack([attn_gain, moe_gain, ffn_gain]).astype(F32)
-        n, route, send = prepare(tp, x, gains, w_router.T, expert_ids[0].T, slot_ids[0].T, experts * sub)
         cos, sin = rope_tables(seq, head_dim)
         flat = lambda w: w.reshape(d_model * heads, head_dim)
-        out = fused_layer(tp, ep, heads, top_k, n, flat(w_query), flat(w_key), flat(w_value), w_out.reshape(heads * head_dim, d_model), x,
-                          gains, w_gate.T, w_up.T, w_down, send,
-                          exp_gate[0].T, exp_up[0].T, exp_down[0], route, cos, sin)
+        out = fused_layer(tp, ep, heads, experts * sub, flat(w_query), flat(w_key), flat(w_value), w_out.reshape(heads * head_dim, d_model), x,
+                          gains, w_gate.T, w_up.T, w_down, exp_gate[0].T, exp_up[0].T, exp_down[0],
+                          w_router.T, expert_ids[0].T, slot_ids[0].T, cos, sin)
         return out[None]
 
     return jax.shard_map(layer_local, mesh=mesh, in_specs=in_specs, out_specs=tok_spec, check_vma=False)

time: 446 us -> 428 us (0.960)
  Pallas kernels: 434 us -> 416 us
    pallas_call x2 -> x1, Pallas kernels: 434 us -> 416 us  [fused_layer(): pl.pallas_call(functools.partial(layer_kernel, tp, ep, heads), out_shape=...]
where the time goes in v3:
time: 428 us; the launch traced here: 427 us
  Pallas kernels  416 us (97%)
  local copies, waits for them, and re-layouts  10 us (2%)
    pallas_call x1, Pallas kernels, fused_layer(): pl.pallas_call(functools.partial(layer_kernel, tp, ep, heads), out_shape=...  416 us

profile of v3, /device:TPU:97, one launch (start us, length us, event | category | flops | bytes accessed | tf_op | source)
XLA Modules:
  0.0 427.1 jit_solution(10423845314462637690)
XLA Ops:
  0.0 0.7 stack.12
  0.7 0.7 stack.14
  1.4 0.7 stack.13
  2.1 0.7 maximum_convert_fusion.gain
  2.8 416.4 %shard_map.181 = (bf16[1024,4096]{1,0:T(8,128)(2,1)}, bf16[1024,4096]{1,0:T(8,128)(2,1)}, bf16[768,4096]{1,0:T(8,128)(2,1)}, bf16[4096,3072]{1,0:T(8,128)(2,1)},...) custom-call(bf16[32768,128]{1,0:T(8,128)(2,1)} %bitcast.28, ...), custom_call_target="tpu_custom_call" | custom-call | flops 69256347648 | bytes 314572800 | tf_op jit(solution)/shard_map/pallas_call | solution.py:715
  419.2 7.9 %copy.21 = bf16[1,1024,4096]{2,1,0:T(8,128)(2,1)} copy(bf16[1,1024,4096]{2,1,0:T(8,128)(2,1)} %bitcast.22) | data formatting | bytes 16777216

commit v4 on v3

--- a/solution.py
+++ b/solution.py
@@ -30,12 +30,14 @@
     row = lax.broadcasted_iota(jnp.int32, (block, block), 0)
     col = lax.broadcasted_iota(jnp.int32, (block, block), 1)
     order = jnp.where(col == (row % span) * heads + row // span, 1.0, 0.0).astype(BF16)
-    for g in range(depth // span):
-        for w, ref in enumerate(sources):
-            moved = jnp.dot(order, ref[g * block:(g + 1) * block, :], preferred_element_type=F32).astype(BF16)
+    pieces = [(g, w) for g in range(depth // span) for w in range(len(sources))]
+    for first, second in zip(pieces[::2], pieces[1::2]):
+        both = jnp.concatenate([sources[w][g * block:(g + 1) * block, :] for g, w in (first, second)], axis=1)
+        moved = jnp.dot(order, both, preferred_element_type=F32).astype(BF16)
+        for part, (g, w) in enumerate((first, second)):
             for k in range(heads):
                 lane = (w * heads + k) * head_dim
-                o_ref[g * span:(g + 1) * span, lane:lane + head_dim] = moved[k * span:(k + 1) * span]
+                o_ref[g * span:(g + 1) * span, lane:lane + head_dim] = moved[k * span:(k + 1) * span, part * head_dim:(part + 1) * head_dim]
     wide = 512
     for t in range(o_ref.shape[1] // wide):
         cols = pl.ds(t * wide, wide)
@@ -50,9 +52,9 @@
 NN_SLOTS = 4
 
 
-def layer_kernel(tp, ep, heads, wq, wk, wv, w_out, x, gain, wg, wu, wd, eg, eu, ed, wr, ids, slots, cos_ref, sin_ref,
+def layer_kernel(tp, ep, heads, wq, wk, wv, w_out, x, gain_flat, wg, wu, wd, eg, eu, ed, wr, ids, slots, cos_ref, sin_ref,
                  out, n, send, wqkv, c_l, c_r, c_o, a_l, a_r, a_o, wx, recv, y, back,
-                 route, r1, r2, a_own, a_mine, out_q, wb1, wb2, wb3,
+                 gain, route, r1, r2, a_own, a_mine, out_q, wb1, wb2, wb3,
                  send_sem, recv_sem, dsend, drecv, ysend, yrecv, ysem, wsend, wrecv, sem1, sem2, sem3, lsem, osem):
     seq, d_model = out.shape
     rows = seq // CHUNKS
@@ -302,6 +304,10 @@
         start(a_second, c)
 
     w_start()
+    lanes = gain_flat.shape[1]
+    per = d_model // lanes
+    for k in range(gain_flat.shape[0]):
+        gain[k // per:k // per + 1, (k % per) * lanes:(k % per + 1) * lanes] = gain_flat[k:k + 1, :]
 
     def prepare(u, pick, x_in, n_out, piled):
         size = x_in.shape[1]
@@ -364,10 +370,10 @@
         for i in range(blocks - 2, blocks):
             n_put(i, i % 2).wait()
 
-    tokens = 128
+    tokens = 256
     pl.run_scoped(
         prepare, pltpu.VMEM((seq, d_model), BF16), pltpu.VMEM((slots_all, seq), BF16), pltpu.VMEM((2, tokens, d_model), BF16),
-        pltpu.VMEM((2, tokens, d_model), BF16), pltpu.VMEM((2, slots_all, 512), BF16))
+        pltpu.VMEM((2, tokens, d_model), BF16), pltpu.VMEM((2, slots_all, 1024), BF16))
     for q in others:
         d_copy(q).start()
 
@@ -719,6 +725,7 @@
         in_specs=[any_spec] * 5 + [vmem_spec] + [any_spec] * 6 + [vmem_spec] * 5,
         out_specs=[any_spec] * 14,
         scratch_shapes=[
+            pltpu.VMEM((3, d_model), F32),
             pltpu.VMEM((8, seq), F32),
             pltpu.VMEM((2, 2, quarter // 2, d_model), F32),
             pltpu.VMEM((2, 2, quarter, d_model), F32),
@@ -765,7 +772,7 @@
         cap = 3 * seq * top_k // (2 * experts)
         sub = cap // tp
         x = hidden_in[0]
-        gains = jnp.stack([attn_gain, moe_gain, ffn_gain]).astype(F32)
+        gains = jnp.concatenate([attn_gain, moe_gain, ffn_gain]).astype(F32).reshape(-1, 128)
         cos, sin = rope_tables(seq, head_dim)
         flat = lambda w: w.reshape(d_model * heads, head_dim)
         out = fused_layer(tp, ep, heads, experts * sub, flat(w_query), flat(w_key), flat(w_value), w_out.reshape(heads * head_dim, d_model), x,

time: 428 us -> 419 us (0.979)
  Pallas kernels: 416 us -> 410 us
    pallas_call x1, Pallas kernels: 416 us -> 410 us  [fused_layer(): pl.pallas_call(functools.partial(layer_kernel, tp, ep, heads), out_shape=...]
where the time goes in v4:
time: 419 us
  Pallas kernels  410 us (98%)
  local copies, waits for them, and re-layouts  7.89 us (2%)
    pallas_call x1, Pallas kernels, fused_layer(): pl.pallas_call(functools.partial(layer_kernel, tp, ep, heads), out_shape=...  410 us

profile of v4, /device:TPU:97, one launch (start us, length us, event | category | flops | bytes accessed | tf_op | source)
XLA Modules:
  0.0 418.8 jit_solution(9886335441964376882)
XLA Ops:
  0.0 1.4 maximum_convert_fusion.gain_flat
  1.4 409.5 %shard_map.181 = (bf16[1024,4096]{1,0:T(8,128)(2,1)}, bf16[1024,4096]{1,0:T(8,128)(2,1)}, bf16[768,4096]{1,0:T(8,128)(2,1)}, bf16[4096,3072]{1,0:T(8,128)(2,1)},...) custom-call(bf16[32768,128]{1,0:T(8,128)(2,1)} %bitcast.34, ...), custom_call_target="tpu_custom_call" | custom-call | flops 69256347648 | bytes 314572800 | tf_op jit(solution)/shard_map/pallas_call | solution.py:721
  410.9 7.9 %copy.21 = bf16[1,1024,4096]{2,1,0:T(8,128)(2,1)} copy(bf16[1,1024,4096]{2,1,0:T(8,128)(2,1)} %bitcast.25) | data formatting | bytes 16777216
